TPU v7x, 32 devices: a whole 2x2x4 slice. The times are simulated.
32 devices in a mesh: gx: 8 (over y, x, core), gy: 4 (over z).
Axes of the slice: x: 2, y: 2, z: 4, core: 2. Of those that a mesh axis runs over, the one named last changes fastest.
Arguments:
- features: bfloat16 [32, 16, 128, 128], P(None, 'gx', 'gy'), may hold values from -80 to 80
- kernel_one: bfloat16 [32, 32, 3, 3, 3], replicated, may hold values from -0.21875 to 0.21875
- gain_one: float32 [32], replicated, may hold values from 0.5 to 1.5
- bias_one: float32 [32], replicated, may hold values from -0.5 to 0.5
- kernel_two: bfloat16 [32, 32, 3, 3, 3], replicated, may hold values from -0.21875 to 0.21875
- gain_two: float32 [32], replicated, may hold values from 0.5 to 1.5
- bias_two: float32 [32], replicated, may hold values from -0.5 to 0.5
- cotangent: bfloat16 [32, 16, 128, 128], P(None, 'gx', 'gy'), may hold values from -80 to 80
Outputs:
- output: bfloat16 [32, 16, 128, 128], P(None, 'gx', 'gy')
- features_grad: bfloat16 [32, 16, 128, 128], P(None, 'gx', 'gy')
- kernel_one_grad: float32 [32, 32, 3, 3, 3], replicated
- kernel_two_grad: float32 [32, 32, 3, 3, 3], replicated
- norm_grads: float32 [4, 32], replicated
All inputs are finite; a program needn't handle non-finite values.
Results may differ from a plain program's by a relative error of at most 0.0078.
Values may be sent and summed in bfloat16 or wider, within the bound.
A program may use at most 192 MiB of HBM per device.

v0:
```python
import functools

import jax
import jax.numpy as jnp
from jax import lax
from jax.experimental import pallas as pl
from jax.experimental.pallas import tpu as pltpu
from jax.sharding import PartitionSpec as P

EPSILON = 1e-05
SLOPE = 0.01
SHARPNESS = 8.0
MESH = pl.DeviceIdType.MESH
F32 = jnp.float32
BF16 = jnp.bfloat16
VSPEC = pl.BlockSpec(memory_space=pltpu.VMEM)
PIECES = 4
DIRECTIONS = [(i, j) for i in (-1, 0, 1) for j in (-1, 0, 1) if (i, j) != (0, 0)]


def activate(shifted):
    scaled = SHARPNESS * shifted
    soft = jnp.maximum(scaled, 0.0) + jnp.log1p(jnp.exp(-jnp.abs(scaled)))
    return SLOPE * shifted + (1.0 - SLOPE) * soft / SHARPNESS


def activate_slope(shifted):
    return SLOPE + (1.0 - SLOPE) / (1.0 + jnp.exp(-SHARPNESS * shifted))


def start_halo(nx, ny, t_ref, p_ref, send, recv):
    gx, gy = lax.axis_index("gx"), lax.axis_index("gy")
    X, Y = t_ref.shape[0], t_ref.shape[1]
    peers = [(lax.rem(gx + dx + nx, nx), lax.rem(gy + dy + ny, ny)) for dx, dy in DIRECTIONS]
    barrier = pltpu.get_barrier_semaphore()
    for peer in peers:
        pl.semaphore_signal(barrier, inc=1, device_id=peer, device_id_type=MESH)
    pl.semaphore_wait(barrier, len(peers))

    def source(d, size):
        return pl.ds(size - 1, 1) if d == 1 else (pl.ds(0, 1) if d == -1 else pl.ds(0, size))

    def target(d, size):
        return pl.ds(0, 1) if d == 1 else (pl.ds(size + 1, 1) if d == -1 else pl.ds(1, size))

    piece = Y // PIECES
    plan = []
    for n in range(PIECES):
        for k, (dx, dy) in enumerate(DIRECTIONS):
            if dy == 0:
                rows_from, rows_to = pl.ds(n * piece, piece), pl.ds(n * piece + 1, piece)
                plan.append((n, k, dx, rows_from, rows_to))
            elif n == 0:
                plan.append((n, k, dx, source(dy, Y), target(dy, Y)))
    groups = [[] for _ in range(PIECES)]
    for index, (n, k, dx, rows_from, rows_to) in enumerate(plan):
        copy = pltpu.make_async_remote_copy(
            src_ref=t_ref.at[source(dx, X), rows_from],
            dst_ref=p_ref.at[target(dx, X), rows_to],
            send_sem=send.at[index],
            recv_sem=recv.at[index],
            device_id=peers[k],
            device_id_type=MESH,
        )
        copy.start()
        groups[n].append(copy)
    return groups


def greet(nx, ny, gx, gy):
    barrier = pltpu.get_barrier_semaphore()
    for k in range(1, nx):
        peer = (lax.rem(gx + k, nx), gy)
        pl.semaphore_signal(barrier, inc=1, device_id=peer, device_id_type=MESH)
    for k in range(1, ny):
        peer = (gx, lax.rem(gy + k, ny))
        pl.semaphore_signal(barrier, inc=1, device_id=peer, device_id_type=MESH)
    pl.semaphore_wait(barrier, nx + ny - 2)


def spread(count, me, peer_of, source_of, slots, send, recv):
    copies = []
    for k in range(1, count):
        other = lax.rem(me + k, count)
        copy = pltpu.make_async_remote_copy(
            src_ref=source_of(other),
            dst_ref=slots(me),
            send_sem=send.at[k],
            recv_sem=recv.at[me],
            device_id=peer_of(other),
            device_id_type=MESH,
        )
        copy.start()
        copies.append(copy)
    for k in range(1, count):
        other = lax.rem(me + k, count)
        pltpu.make_async_remote_copy(
            src_ref=source_of(other),
            dst_ref=slots(other),
            send_sem=send.at[k],
            recv_sem=recv.at[other],
            device_id=peer_of(other),
            device_id_type=MESH,
        ).wait_recv()
    for copy in copies:
        copy.wait_send()


def ordered_sum(ref, count):
    total = ref[0]
    for k in range(1, count):
        total = total + ref[k]
    return total


def stats_kernel(nx, ny, s_ref, o_ref, bx, by, mid, sx, rx, sy, ry):
    gx, gy = lax.axis_index("gx"), lax.axis_index("gy")
    greet(nx, ny, gx, gy)
    bx[gx] = s_ref[...]
    spread(nx, gx, lambda o: (o, gy), lambda o: s_ref, lambda i: bx.at[i], sx, rx)
    mid[...] = ordered_sum(bx, nx)
    by[gy] = mid[...]
    spread(ny, gy, lambda o: (gx, o), lambda o: mid, lambda i: by.at[i], sy, ry)
    o_ref[...] = ordered_sum(by, ny)


def sum_stats(local, nx, ny):
    R, L = local.shape
    return pl.pallas_call(
        functools.partial(stats_kernel, nx, ny),
        name="stats_sum",
        out_shape=jax.ShapeDtypeStruct((R, L), F32),
        in_specs=[VSPEC],
        out_specs=VSPEC,
        scratch_shapes=[
            pltpu.VMEM((nx, R, L), F32),
            pltpu.VMEM((ny, R, L), F32),
            pltpu.VMEM((R, L), F32),
            pltpu.SemaphoreType.DMA((nx,)),
            pltpu.SemaphoreType.DMA((nx,)),
            pltpu.SemaphoreType.DMA((ny,)),
            pltpu.SemaphoreType.DMA((ny,)),
        ],
        compiler_params=pltpu.CompilerParams(collective_id=1, has_side_effects=True),
    )(local)


def weights_kernel(nx, ny, s_ref, o_ref, bx, by, mid, fin, gat, sx, rx, sy, ry, sg, rg):
    gx, gy = lax.axis_index("gx"), lax.axis_index("gy")
    greet(nx, ny, gx, gy)
    bx[gx] = s_ref[gx]
    spread(nx, gx, lambda o: (o, gy), lambda o: s_ref.at[o], lambda i: bx.at[i], sx, rx)
    mid[...] = ordered_sum(bx, nx)
    by[gy] = mid[...]
    spread(ny, gy, lambda o: (gx, o), lambda o: mid, lambda i: by.at[i], sy, ry)
    fin[...] = ordered_sum(by, ny)
    gat[gx] = fin[...]
    spread(nx, gx, lambda o: (o, gy), lambda o: fin, lambda i: gat.at[i], sg, rg)
    o_ref[...] = gat[...]


def sum_weights(local, nx, ny):
    R, L = local.shape
    piece = -(-R // (8 * nx)) * 8
    split = jnp.pad(local, ((0, piece * nx - R), (0, 0))).reshape(nx, piece, L)
    summed = pl.pallas_call(
        functools.partial(weights_kernel, nx, ny),
        name="weights_sum",
        out_shape=jax.ShapeDtypeStruct((nx, piece, L), F32),
        in_specs=[VSPEC],
        out_specs=VSPEC,
        scratch_shapes=[
            pltpu.VMEM((nx, piece, L), F32),
            pltpu.VMEM((ny, piece, L), F32),
            pltpu.VMEM((piece, L), F32),
            pltpu.VMEM((piece, L), F32),
            pltpu.VMEM((nx, piece, L), F32),
            pltpu.SemaphoreType.DMA((nx,)),
            pltpu.SemaphoreType.DMA((nx,)),
            pltpu.SemaphoreType.DMA((ny,)),
            pltpu.SemaphoreType.DMA((ny,)),
            pltpu.SemaphoreType.DMA((nx,)),
            pltpu.SemaphoreType.DMA((nx,)),
        ],
        compiler_params=pltpu.CompilerParams(collective_id=2, has_side_effects=True),
    )(split)
    return summed.reshape(nx * piece, L)[:R]


def taps(row, flip, keep=None):
    wide = row.astype(F32)
    if keep is not None:
        wide = wide * keep
        row = wide.astype(BF16)
    size = row.shape[1]
    lane = lax.broadcasted_iota(jnp.int32, wide.shape, 1)
    before = jnp.where(lane == 0, 0.0, pltpu.roll(wide, 1, 1)).astype(BF16)
    after = jnp.where(lane == size - 1, 0.0, pltpu.roll(wide, size - 1, 1)).astype(BF16)
    return jnp.concatenate([after, row, before] if flip else [before, row, after], axis=0)


def conv_halo(nx, ny, flip, t_ref, w_ref, acc_ref, p_ref, send, recv, v_ref=None, dw_ref=None):
    X, _, C, Z = acc_ref.shape
    Y = t_ref.shape[1]
    gx, gy = lax.axis_index("gx"), lax.axis_index("gy")
    groups = start_halo(nx, ny, t_ref, p_ref, send, recv)
    acc_ref[...] = jnp.zeros_like(acc_ref)
    if dw_ref is not None:
        dw_ref[...] = jnp.zeros(dw_ref.shape, F32)

    def pair_step(xp, ya, yb, tap_a, tap_b):
        first, last = max(0, xp - (X - 1)), min(2, xp)
        blocks = range(2 - last, 3 - first) if flip else range(first, last + 1)
        low, high = blocks[0] * 3 * C, (blocks[-1] + 1) * 3 * C
        pair = jnp.concatenate([tap_a, tap_b], axis=1)
        part = jnp.dot(w_ref[low:high, :], pair, preferred_element_type=F32)
        left = []
        for n, block in enumerate(blocks):
            x = xp - 2 + block if flip else xp - block
            base = n * 3 * C
            one = [part[base + d * C : base + (d + 1) * C, :Z] for d in range(3)]
            two = [part[base + d * C : base + (d + 1) * C, Z:] for d in range(3)]
            if not flip:
                one, two = one[::-1], two[::-1]
            if yb is None:
                acc_ref[x, ya] += one[0]
                acc_ref[x, ya + 1] += one[1] + two[0]
                acc_ref[x, ya + 2] += one[2] + two[1]
                acc_ref[x, ya + 3] += two[2]
            else:
                for d in range(3):
                    acc_ref[x, ya + d] += one[d]
                for d in range(3):
                    acc_ref[x, yb + d] += two[d]
            if dw_ref is not None:
                second = ya + 1 if yb is None else yb
                now = v_ref[x, pl.ds(ya, 3)].reshape(3 * C, Z)
                later = v_ref[x, pl.ds(second, 3)].reshape(3 * C, Z)
                left.append(jnp.concatenate([now, later], axis=1))
        if dw_ref is not None:
            left = left[0] if len(left) == 1 else jnp.concatenate(left, axis=0)
            dw_ref[low:high, : 3 * C] += lax.dot_general(
                left, pair, (((1,), (1,)), ((), ())), preferred_element_type=F32
            )

    def inner(j, carry):
        y = 2 * j + 1
        for xp in range(1, X + 1):
            tap_a = taps(t_ref[xp - 1, y - 1], flip)
            tap_b = taps(t_ref[xp - 1, y], flip)
            pair_step(xp, y, None, tap_a, tap_b)
        return carry

    lax.fori_loop(0, Y // 2, inner, 0)
    for copy in groups[0]:
        copy.wait()
    low_y = jnp.where(gy > 0, 1.0, 0.0)
    high_y = jnp.where(gy < ny - 1, 1.0, 0.0)
    for xp in range(1, X + 1):
        tap_a = taps(p_ref[xp, 0], flip, low_y)
        tap_b = taps(p_ref[xp, Y + 1], flip, high_y)
        pair_step(xp, 0, Y + 1, tap_a, tap_b)
    low_x = jnp.where(gx > 0, 1.0, 0.0)
    high_x = jnp.where(gx < nx - 1, 1.0, 0.0)

    def outer(j, carry):
        y = 2 * j
        keep_a = jnp.where(y == 0, low_y, 1.0)
        keep_b = jnp.where(y == Y, high_y, 1.0)
        for xp, keep in ((0, low_x), (X + 1, high_x)):
            tap_a = taps(p_ref[xp, y], flip, keep * keep_a)
            tap_b = taps(p_ref[xp, y + 1], flip, keep * keep_b)
            pair_step(xp, y, None, tap_a, tap_b)
        return carry

    done = 0
    for n, group in enumerate(groups):
        if n > 0:
            for copy in group:
                copy.wait()
        ready = (Y + 2) // 2 if n == PIECES - 1 else (Y // PIECES * (n + 1) + 1) // 2
        lax.fori_loop(done, ready, outer, 0)
        done = ready


def pack_pair(one, two):
    C = one.shape[0]
    lane = lax.broadcasted_iota(jnp.int32, one.shape, 1)
    one = jnp.sum(one, axis=1, keepdims=True)
    two = jnp.sum(two, axis=1, keepdims=True)
    tall = jnp.where(lane == 0, one, jnp.where(lane == 1, two, 0.0))
    square = jnp.concatenate([tall, jnp.zeros((128 - C, 128), F32)], axis=0)
    return jnp.transpose(square)[0:8]


def unpack_pair(s_ref, C):
    square = jnp.concatenate([s_ref[...], jnp.zeros((120, 128), F32)], axis=0)
    tall = jnp.transpose(square)
    return tall[:C, 0:1], tall[:C, 1:2]


def normal_terms(s_ref, C, total_cells):
    sums, squares = unpack_pair(s_ref, C)
    center = sums / total_cells
    spread_ = squares / total_cells - jnp.square(center)
    return center, lax.rsqrt(spread_ + EPSILON)


def rows(X, Y, step, carry):
    group = 4 if Y % 4 == 0 else 1

    def body(block, carry):
        for k in range(group):
            for x in range(X):
                carry = step(x, block * group + k, carry)
        return carry

    return lax.fori_loop(0, Y // group, body, carry)


def forward_kernel(nx, ny, t_ref, w_ref, h_ref, s_ref, acc_ref, p_ref, send, recv):
    X, Y, C, Z = h_ref.shape
    conv_halo(nx, ny, False, t_ref, w_ref, acc_ref, p_ref, send, recv)

    def step(x, y, carry):
        h = acc_ref[x, y + 2]
        h_ref[x, y] = h
        return carry[0] + h, carry[1] + h * h

    zero = jnp.zeros((C, Z), F32)
    s_ref[...] = pack_pair(*rows(X, Y, step, (zero, zero)))


def active_kernel(total_cells, h_ref, s_ref, gb_ref, a_ref):
    X, Y, C, Z = h_ref.shape
    center, inverse = normal_terms(s_ref, C, total_cells)
    gain, bias = gb_ref[0], gb_ref[1]

    def step(x, y, carry):
        shifted = (h_ref[x, y] - center) * inverse * gain + bias
        a_ref[x, y] = activate(shifted).astype(BF16)
        return carry

    rows(X, Y, step, 0)


def output_kernel(total_cells, h_ref, s_ref, gb_ref, c_ref, o_ref, t_ref):
    X, Y, C, Z = h_ref.shape
    center, inverse = normal_terms(s_ref, C, total_cells)
    gain, bias = gb_ref[0], gb_ref[1]

    def step(x, y, carry):
        normed = (h_ref[x, y] - center) * inverse
        shifted = normed * gain + bias
        o_ref[x, y] = activate(shifted).astype(BF16)
        slope = c_ref[x, y].astype(F32) * activate_slope(shifted)
        return carry[0] + slope, carry[1] + slope * normed

    zero = jnp.zeros((C, Z), F32)
    t_ref[...] = pack_pair(*rows(X, Y, step, (zero, zero)))


def gradient_kernel(total_cells, has_slope, h_ref, s_ref, gb_ref, c_ref, t_ref, g_ref):
    X, Y, C, Z = h_ref.shape
    center, inverse = normal_terms(s_ref, C, total_cells)
    gain, bias = gb_ref[0], gb_ref[1]
    plain, along = [v / total_cells for v in unpack_pair(t_ref, C)]
    factor = gain * inverse

    def step(x, y, carry):
        normed = (h_ref[x, y] - center) * inverse
        slope = c_ref[x, y].astype(F32)
        if not has_slope:
            slope = slope * activate_slope(normed * gain + bias)
        g_ref[x, y] = (factor * (slope - plain - normed * along)).astype(BF16)
        return carry

    rows(X, Y, step, 0)


def fill_own(v_ref, own_ref):
    X, Y, C, Z = v_ref.shape
    edge = jnp.zeros((X, 2, C, Z), BF16)
    own_ref[:, 0:2] = edge
    own_ref[:, Y + 2 : Y + 4] = edge
    own_ref[:, 2 : Y + 2] = v_ref[...]


def back_kernel(
    total_cells, nx, ny, g_ref, v_ref, w_ref, h_ref, s_ref, gb_ref,
    o_ref, t_ref, dw_ref, acc_ref, p_ref, send, recv, own_ref,
):
    X, Y, C, Z = o_ref.shape
    fill_own(v_ref, own_ref)
    conv_halo(nx, ny, True, g_ref, w_ref, acc_ref, p_ref, send, recv, own_ref, dw_ref)
    center, inverse = normal_terms(s_ref, C, total_cells)
    gain, bias = gb_ref[0], gb_ref[1]

    def step(x, y, carry):
        normed = (h_ref[x, y] - center) * inverse
        slope = acc_ref[x, y + 2] * activate_slope(normed * gain + bias)
        o_ref[x, y] = slope
        return carry[0] + slope, carry[1] + slope * normed

    zero = jnp.zeros((C, Z), F32)
    t_ref[...] = pack_pair(*rows(X, Y, step, (zero, zero)))


def last_kernel(
    nx, ny, g_ref, v_ref, w_ref, d_ref, o_ref, both_ref, acc_ref, p_ref, send, recv, own_ref
):
    X, Y, C, Z = o_ref.shape
    fill_own(v_ref, own_ref)
    both_ref[9 * C :] = d_ref[...]
    dw_ref = both_ref.at[0 : 9 * C]
    conv_halo(nx, ny, True, g_ref, w_ref, acc_ref, p_ref, send, recv, own_ref, dw_ref)

    def step(x, y, carry):
        o_ref[x, y] = acc_ref[x, y + 2].astype(BF16)
        return carry

    rows(X, Y, step, 0)


def call(kernel, name, outs, *operands, scratch=(), collective=None):
    params = {}
    if collective is not None:
        params["compiler_params"] = pltpu.CompilerParams(
            collective_id=collective, has_side_effects=True
        )
    return pl.pallas_call(
        kernel,
        name=name,
        out_shape=[jax.ShapeDtypeStruct(s, d) for s, d in outs],
        in_specs=[VSPEC] * len(operands),
        out_specs=[VSPEC] * len(outs),
        scratch_shapes=list(scratch),
        **params,
    )(*operands)


def local(features, kernel_one, gain_one, bias_one, kernel_two, gain_two, bias_two, cotangent):
    C, X, Y, Z = features.shape
    nx, ny = lax.axis_size("gx"), lax.axis_size("gy")
    total_cells = float(X * Y * Z * nx * ny)
    full = (X, Y, C, Z)
    tall = (X, Y + 4, C, Z)
    stat = (8, 128)
    faces = [
        pltpu.VMEM(tall, F32),
        pltpu.VMEM((X + 2, Y + 2, C, Z), BF16),
        pltpu.SemaphoreType.DMA((6 + 2 * PIECES,)),
        pltpu.SemaphoreType.DMA((6 + 2 * PIECES,)),
    ]
    own = [pltpu.VMEM(tall, BF16)]
    forward = functools.partial(forward_kernel, nx, ny)

    def ahead(kernel):
        return jnp.transpose(kernel, (2, 3, 0, 4, 1)).reshape(9 * C, 3 * C)

    def behind(kernel):
        return jnp.transpose(kernel, (2, 3, 1, 4, 0)).reshape(9 * C, 3 * C)

    def rows_of(gain, bias):
        return jnp.broadcast_to(jnp.stack([gain, bias])[:, :, None], (2, C, Z))

    params_one, params_two = rows_of(gain_one, bias_one), rows_of(gain_two, bias_two)
    ft = jnp.transpose(features, (1, 2, 0, 3))
    ct = jnp.transpose(cotangent, (1, 2, 0, 3))

    h1, s1 = call(
        forward, "forward", [(full, F32), (stat, F32)], ft, ahead(kernel_one),
        scratch=faces, collective=0,
    )
    s1 = sum_stats(s1, nx, ny)
    (a,) = call(
        functools.partial(active_kernel, total_cells), "active", [(full, BF16)], h1, s1, params_one
    )
    h2, s2 = call(
        forward, "forward", [(full, F32), (stat, F32)], a, ahead(kernel_two),
        scratch=faces, collective=0,
    )
    s2 = sum_stats(s2, nx, ny)
    out, t2 = call(
        functools.partial(output_kernel, total_cells), "output", [(full, BF16), (stat, F32)],
        h2, s2, params_two, ct,
    )
    t2 = sum_stats(t2, nx, ny)
    (g2,) = call(
        functools.partial(gradient_kernel, total_cells, False), "grad_two", [(full, BF16)],
        h2, s2, params_two, ct, t2,
    )
    slope_one, t1, dw2 = call(
        functools.partial(back_kernel, total_cells, nx, ny), "back",
        [(full, F32), (stat, F32), ((9 * C, 128), F32)],
        g2, a, behind(kernel_two), h1, s1, params_one,
        scratch=faces + own, collective=3,
    )
    t1 = sum_stats(t1, nx, ny)
    (g1,) = call(
        functools.partial(gradient_kernel, total_cells, True), "grad_one", [(full, BF16)],
        h1, s1, params_one, slope_one, t1,
    )
    fg, dw = call(
        functools.partial(last_kernel, nx, ny), "last", [(full, BF16), ((18 * C, 128), F32)],
        g1, ft, behind(kernel_one), dw2, scratch=faces + own, collective=4,
    )
    summed = sum_weights(dw, nx, ny)
    scale = 1.0 / jnp.sqrt(jnp.float32(total_cells))

    def gradient_of(block):
        split = block[:, : 3 * C].reshape(3, 3, C, 3, C)
        return jnp.transpose(split, (4, 2, 0, 1, 3)) * scale

    norm_grads = jnp.stack([t1[1, :C], t1[0, :C], t2[1, :C], t2[0, :C]]) * scale
    return (
        jnp.transpose(out, (2, 0, 1, 3)),
        jnp.transpose(fg, (2, 0, 1, 3)),
        gradient_of(summed[: 9 * C]),
        gradient_of(summed[9 * C :]),
        norm_grads,
    )


def solution(mesh):
    in_specs = (P(None, "gx", "gy", None), P(), P(), P(), P(), P(), P(), P(None, "gx", "gy", None))
    out_specs = (P(None, "gx", "gy", None), P(None, "gx", "gy", None), P(), P(), P())
    return jax.shard_map(local, mesh=mesh, in_specs=in_specs, out_specs=out_specs, check_vma=False)
```

profile of v0, /device:TPU:0, one launch (start us, length us, event | category | flops | bytes accessed | tf_op | source)
XLA Modules:
  0.0 154.4 jit_solution(14142473574288473106)
XLA Ops:
  0.6 2.2 %copy.34 = bf16[32,2,32,128]{3,0,2,1:T(8,128)(2,1)} copy(bf16[32,2,32,128]{3,2,1,0:T(8,128)(2,1)} %param.8) | data formatting | bytes 1048576 | tf_op args[0]
  3.0 0.8 reshape.36.w_ref
  3.8 17.7 %forward.2 = (f32[2,32,32,128]{3,2,1,0:T(8,128)}, f32[8,128]{1,0:T(8,128)}) custom-call(bf16[2,32,32,128]{3,2,1,0:T(8,128)(2,1)} %bitcast.21, bf16[288,96]{1,0:T(8,128)(2,1)} %reshape.36.w_ref), custom_call_target="tpu_custom_call" | custom-call | tf_op jit(solution)/shard_map/forward/pallas_call | solution.py:431
  21.5 10.2 %stats_sum.4.s_ref = f32[8,128]{1,0:T(8,128)} custom-call(f32[8,128]{1,0:T(8,128)} %get-tuple-element.17.s_ref), custom_call_target="tpu_custom_call" | custom-call | tf_op jit(solution)/shard_map/stats_sum/pallas_call | solution.py:129
  33.1 3.7 %active.1.t_ref.v_ref = bf16[2,32,32,128]{3,2,1,0:T(8,128)(2,1)} custom-call(f32[2,32,32,128]{3,2,1,0:T(8,128)} %get-tuple-element.16.h_ref, f32[8,128]{1,0:T(8,128)} %stats_sum.4.s_ref, f32[2,32,128]{2,1,0:T(8,128)} %broadcast_in_dim.4.gb_ref), custom_call_target="tpu_custom_call" | custom-call | tf_op jit(solution)/shard_map/active/pallas_call | solution.py:431
  36.9 0.8 reshape.37.w_ref
  37.7 14.5 %forward.3 = (f32[2,32,32,128]{3,2,1,0:T(8,128)}, f32[8,128]{1,0:T(8,128)}) custom-call(bf16[2,32,32,128]{3,2,1,0:T(8,128)(2,1)} %active.1.t_ref.v_ref, bf16[288,96]{1,0:T(8,128)(2,1)} %reshape.37.w_ref), custom_call_target="tpu_custom_call" | custom-call | tf_op jit(solution)/shard_map/forward/pallas_call | solution.py:431
  52.3 9.7 %stats_sum.5.s_ref = f32[8,128]{1,0:T(8,128)} custom-call(f32[8,128]{1,0:T(8,128)} %get-tuple-element.19.s_ref), custom_call_target="tpu_custom_call" | custom-call | tf_op jit(solution)/shard_map/stats_sum/pallas_call | solution.py:129
  62.0 1.2 copy.33
  64.5 4.3 %output.1 = (bf16[2,32,32,128]{3,2,1,0:T(8,128)(2,1)}, f32[8,128]{1,0:T(8,128)}) custom-call(f32[2,32,32,128]{3,2,1,0:T(8,128)} %get-tuple-element.18.h_ref, f32[8,128]{1,0:T(8,128)} %stats_sum.5.s_ref, f32[2,32,128]{2,1,0:T(8,128)} %broadcast_in_dim.5.gb_ref, bf16[2,32,32,128]{3,2,1,0:T(8,128)(2,1)} %bitcast.23), custom_call_target="tpu_custom_call" | custom-call | tf_op jit(solution)/shard_map/output/pallas_call | solution.py:431
  68.8 10.3 %stats_sum.6.t_ref = f32[8,128]{1,0:T(8,128)} custom-call(f32[8,128]{1,0:T(8,128)} %get-tuple-element.21.s_ref), custom_call_target="tpu_custom_call" | custom-call | tf_op jit(solution)/shard_map/stats_sum/pallas_call | solution.py:129
  79.1 3.7 %grad_two.1.g_ref = bf16[2,32,32,128]{3,2,1,0:T(8,128)(2,1)} custom-call(f32[2,32,32,128]{3,2,1,0:T(8,128)} %get-tuple-element.18.h_ref, f32[8,128]{1,0:T(8,128)} %stats_sum.5.s_ref, f32[2,32,128]{2,1,0:T(8,128)} %broadcast_in_dim.5.gb_ref, bf16[2,32,32,128]{3,2,1,0:T(8,128)(2,1)} %bitcast.24, f32[8,128]{1,0:T(8,128)} %stats_sum.6.t_ref), custom_call_target="tpu_custom_call" | custom-call | tf_op jit(solution)/shard_map/grad_two/pallas_call | solution.py:431
  83.0 0.8 reshape.38.w_ref
  83.8 16.7 %back.1 = (f32[2,32,32,128]{3,2,1,0:T(8,128)}, f32[8,128]{1,0:T(8,128)}, f32[288,128]{1,0:T(8,128)}) custom-call(bf16[2,32,32,128]{3,2,1,0:T(8,128)(2,1)} %grad_two.1.g_ref, bf16[2,32,32,128]{3,2,1,0:T(8,128)(2,1)} %active.1.t_ref.v_ref, bf16[288,96]{1,0:T(8,128)(2,1)} %reshape.38.w_ref, f32[2,32,32,128]{3,2,1,0:T(8,128)} %get-tuple-element.16.h_ref, ...), custom_call_target="tpu_custom_call" | custom-call | tf_op jit(solution)/shard_map/back/pallas_call | solution.py:431
  100.5 9.7 %stats_sum.7.t_ref = f32[8,128]{1,0:T(8,128)} custom-call(f32[8,128]{1,0:T(8,128)} %get-tuple-element.23.s_ref), custom_call_target="tpu_custom_call" | custom-call | tf_op jit(solution)/shard_map/stats_sum/pallas_call | solution.py:129
  111.6 3.4 %grad_one.1.g_ref = bf16[2,32,32,128]{3,2,1,0:T(8,128)(2,1)} custom-call(f32[2,32,32,128]{3,2,1,0:T(8,128)} %get-tuple-element.16.h_ref, f32[8,128]{1,0:T(8,128)} %stats_sum.4.s_ref, f32[2,32,128]{2,1,0:T(8,128)} %broadcast_in_dim.4.gb_ref, f32[2,32,32,128]{3,2,1,0:T(8,128)} %get-tuple-element.22.c_ref, f32[8,128]{1,0:T(8,128)} %stats_sum.7.t_ref), custom_call_target="tpu_custom_call" | custom-call | tf_op jit(solution)/shard_map/grad_one/pallas_call | solution.py:431
  115.3 0.8 reshape.39.w_ref
  116.1 15.4 %last.1 = (bf16[2,32,32,128]{3,2,1,0:T(8,128)(2,1)}, f32[576,128]{1,0:T(8,128)}) custom-call(bf16[2,32,32,128]{3,2,1,0:T(8,128)(2,1)} %grad_one.1.g_ref, bf16[2,32,32,128]{3,2,1,0:T(8,128)(2,1)} %bitcast.22, bf16[288,96]{1,0:T(8,128)(2,1)} %reshape.39.w_ref, f32[288,128]{1,0:T(8,128)} %get-tuple-element.24.d_ref), custom_call_target="tpu_custom_call" | custom-call | tf_op jit(solution)/shard_map/last/pallas_call | solution.py:431
  131.5 17.4 %weights_sum.1 = f32[8,72,128]{2,1,0:T(8,128)} custom-call(f32[8,72,128]{2,1,0:T(8,128)} %bitcast.35), custom_call_target="tpu_custom_call" | custom-call | tf_op jit(solution)/shard_map/weights_sum/pallas_call | solution.py:166
  148.8 1.0 fusion
  150.1 1.0 copy.29
  151.3 1.0 copy.30
  152.4 1.0 copy.28
  153.4 1.0 copy.27
  (32 shorter events, 5.4 us)
Async XLA Ops:
  0.6 2.2 %copy-start.1 = (bf16[32,32,3,3,3]{1,0,4,3,2:T(8,128)(2,1)S(1)}, bf16[32,32,3,3,3]{1,0,4,3,2:T(8,128)(2,1)}, u32[]{:S(2)}) copy-start(bf16[32,32,3,3,3]{1,0,4,3,2:T(8,128)(2,1)} %param.9) | copy-start | bytes 165892
  31.7 0.7 copy-start.5
  31.7 0.7 copy-start.6
  33.1 3.7 %copy-start = (bf16[32,32,3,3,3]{1,0,4,3,2:T(8,128)(2,1)S(1)}, bf16[32,32,3,3,3]{1,0,4,3,2:T(8,128)(2,1)}, u32[]{:S(2)}) copy-start(bf16[32,32,3,3,3]{1,0,4,3,2:T(8,128)(2,1)} %param.12) | copy-start | bytes 165892
  36.9 25.0 %copy-start.2 = (bf16[32,2,32,128]{3,2,1,0:T(8,128)(2,1)S(1)}, bf16[32,2,32,128]{3,2,1,0:T(8,128)(2,1)}, u32[]{:S(2)}) copy-start(bf16[32,2,32,128]{3,2,1,0:T(8,128)(2,1)} %param.15) | copy-start | bytes 1572868
  63.1 0.7 copy-start.7
  63.1 0.7 copy-start.8
  151.3 1.0 copy-start.4
  152.4 1.0 copy-start.3
where the time goes:
time: 155 us; the launch traced here: 154 us
  Pallas kernels  137 us (88%)
  local copies, waits for them, and re-layouts  16.3 us (11%)
    pallas_call x8, Pallas kernels, call(): pl.pallas_call(kernel, name=name, out_shape=[jax.ShapeDtypeStruct(s, d) f...  79.4 us
    pallas_call x4, Pallas kernels, sum_stats(): pl.pallas_call(functools.partial(stats_kernel, nx, ny), name='stats_sum',...  39.9 us
    pallas_call x1, Pallas kernels, sum_weights(): pl.pallas_call(functools.partial(weights_kernel, nx, ny), name='weights_s...  17.4 us
    unnamed x24, local copies, waits for them, and re-layouts  8.74 us

commit v1 on v0

v1 whole, which is shorter than its diff:
```python
import functools

import jax
import jax.numpy as jnp
from jax import lax
from jax.experimental import pallas as pl
from jax.experimental.pallas import tpu as pltpu
from jax.sharding import PartitionSpec as P

EPSILON = 1e-05
SLOPE = 0.01
SHARPNESS = 8.0
MESH = pl.DeviceIdType.MESH
F32 = jnp.float32
BF16 = jnp.bfloat16
L = 128
CH = 4
FEAT, COT, HID1, HID2, SLO1 = range(5)
NEXCH = 5
NT = (((1,), (1,)), ((), ()))


def activate(s):
    scaled = SHARPNESS * s
    soft = jnp.maximum(scaled, 0.0) + jnp.log(1.0 + jnp.exp(-jnp.abs(scaled)))
    return SLOPE * s + ((1.0 - SLOPE) / SHARPNESS) * soft


def activate_slope(s):
    half = 0.5 * (1.0 - SLOPE)
    return (SLOPE + half) + half * jnp.tanh((0.5 * SHARPNESS) * s)


def kernel(
    nx, ny, total,
    f_ref, c_ref, k1_ref, k2_ref, g1_ref, b1_ref, g2_ref, b2_ref,
    o_ref, fg_ref, dk1_ref, dk2_ref, ng_ref,
    t1, par, e_mat, s_mat, i_mat, base, wf1, wf2, wb2, wb1,
    vo_f, vh_f, vo_c, vh_c, vo_a, vh_a, vo_g, vh_g, vt_f, vt_a,
    hc1, hc2, n1o, n1h, n2o, n2h, s2o, s2h, s1o, outb, bs, mcs, scs, mcs1, raw,
    spr, spl, se, rl, rr, re, rdl, rdr, hs_sem, hr_sem,
    msg, st, ss_sem, sr_sem,
    pk, rsb, ags, agb, ws_sem, wr_sem,
):
    C, X, Y, Z = f_ref.shape
    R = Z // 2
    CR = CH * R
    NCH = Y // CH
    n = nx * ny
    PIECE = rsb.shape[2]
    gx, gy = lax.axis_index("gx"), lax.axis_index("gy")
    me = gx * ny + gy
    has_l, has_r = gx > 0, gx < nx - 1
    has_d, has_u = gy > 0, gy < ny - 1

    def coords(d):
        return (d // ny, lax.rem(d, ny))

    barrier = pltpu.get_barrier_semaphore()

    def hello(k, carry):
        pl.semaphore_signal(
            barrier, inc=1, device_id=coords(lax.rem(me + k, n)), device_id_type=MESH
        )
        return carry

    lax.fori_loop(1, n, hello, 0)

    lane = lax.broadcasted_iota(jnp.int32, (1, L), 1)
    xb = lax.rem(lane // C, 2) == 1
    z0 = lane < L // 2
    flag = lambda b: jnp.where(b, 1, 0)
    keep_h = jnp.where(xb, flag(has_l), flag(has_r)) > 0
    full_y = jnp.full((1, L), 1, jnp.int32)
    keep_o = [full_y * flag(has_d) > 0, full_y * flag(has_u) > 0]
    keep_ho = [(jnp.where(xb, flag(has_l), flag(has_r)) * flag(b)) > 0 for b in (has_d, has_u)]

    def row_of(y):
        return pl.multiple_of(y * R, R)

    def fold(v):
        v = v + pltpu.roll(v, C, 1)
        return v + pltpu.roll(v, 2 * C, 1)

    def eight(v):
        return jnp.sum(v.reshape(v.shape[0] // 8, 8, L), axis=0)

    def one(v):
        return jnp.sum(v, axis=0, keepdims=True)

    r_i = lax.broadcasted_iota(jnp.int32, (R, 2 * Z), 0)
    c_i = lax.broadcasted_iota(jnp.int32, (R, 2 * Z), 1)
    e_mat[...] = jnp.where(
        lax.rem(c_i, Z) == 2 * r_i + c_i // Z, 1.0, 0.0
    ).astype(BF16)
    r_i = lax.broadcasted_iota(jnp.int32, (2 * L, 2 * Z), 0)
    c_i = lax.broadcasted_iota(jnp.int32, (2 * L, 2 * Z), 1)
    same = lax.rem(r_i // R, 2) == c_i // Z
    s_mat[...] = jnp.where(
        same & (lax.rem(c_i, Z) == 2 * lax.rem(r_i, R) + r_i // L), 1.0, 0.0
    ).astype(BF16)
    r_i = lax.broadcasted_iota(jnp.int32, (L, L), 0)
    c_i = lax.broadcasted_iota(jnp.int32, (L, L), 1)
    i_mat[...] = jnp.where(r_i == c_i, 1.0, 0.0).astype(BF16)
    par[...] = jnp.zeros(par.shape, F32)
    for row, ref in enumerate((g1_ref, b1_ref, g2_ref, b2_ref)):
        par[row : row + 1, 0:C] = ref[...]
    params = fold(par[...])
    gain1, bias1, gain2, bias2 = [params[r : r + 1] for r in range(4)]
    bs[...] = jnp.zeros(bs.shape, F32)

    spots_in = [(0, 0, z, x) for z in range(2) for x in range(2)]
    halo_x = {0: 2, 1: -1}
    rows_in = [(x, z) for _, _, z, x in spots_in] + [(halo_x[x], z) for _, _, z, x in spots_in]
    cols_a = [(x, z) for _, _, z, x in spots_in]
    cols_b = [(x, 2 if z == 0 else -1) for _, _, z, x in spots_in]

    def build(k_ref, w_ref, forward):
        if forward:
            stacked = jnp.concatenate([k_ref[t] for t in range(27) for _ in range(4)], axis=0)
            wide = lax.dot_general(
                i_mat[0:C, 0:C], stacked, NT, preferred_element_type=F32
            )
            for t in range(27):
                base[t] = wide[:, t * L : (t + 1) * L]
        else:
            r4 = lax.broadcasted_iota(jnp.int32, (C, L), 0)
            c4 = lax.rem(lax.broadcasted_iota(jnp.int32, (C, L), 1), C)
            spread4 = jnp.where(r4 == c4, 1.0, 0.0).astype(BF16)
            tall = k_ref[...].reshape(27 * C, C)
            wide = jnp.dot(tall, spread4, preferred_element_type=F32)
            for t in range(27):
                base[t] = wide[t * C : (t + 1) * C]
        block = lax.broadcasted_iota(jnp.int32, (C, L), 1) // C

        def one_row(j, carry):
            dy = j if forward else 2 - j
            for kb, (xi, zi) in enumerate(rows_in):
                for t, cols in enumerate((cols_a, cols_b)):
                    value = jnp.zeros((C, L), F32)
                    for b, (xo, zo) in enumerate(cols):
                        dx, dz = xi - xo + 1, zi - zo + 1
                        if not forward:
                            dx, dz = 2 - dx, 2 - dz
                        if 0 <= dx <= 2 and 0 <= dz <= 2:
                            tap = base[dx * 9 + dy * 3 + dz]
                            value = jnp.where(block == b, tap, value)
                    w_ref[j, kb * C : (kb + 1) * C, t * L : (t + 1) * L] = value.astype(BF16)
            return carry

        lax.fori_loop(0, 3, one_row, 0)

    def enter(in_ref, vo, e):
        def widen(c, carry):
            t1[pl.ds(pl.multiple_of(c * X * Y, X * Y), X * Y), :] = (
                in_ref[c].reshape(X * Y, Z).astype(F32)
            )
            return carry

        lax.fori_loop(0, C, widen, 0)
        zero = jnp.zeros((X * C, Z), BF16)

        def chunk(c, carry):
            vs = []
            for k in range(CH):
                y = c * CH + k
                x0 = t1[pl.ds(y, C, stride=X * Y), :]
                x1 = t1[pl.ds(Y + y, C, stride=X * Y), :]
                xy = jnp.concatenate([x0, x1], axis=0).astype(BF16)
                rhs = jnp.concatenate(
                    [jnp.concatenate([xy, zero], axis=1), jnp.concatenate([zero, xy], axis=1)],
                    axis=0,
                )
                v = lax.dot_general(e_mat[...], rhs, NT, preferred_element_type=F32)
                vo[pl.ds(row_of(y + 1), R), :] = v.astype(BF16)
                vs.append(v)
            pack(e, c, vs, None)
            return carry

        lax.fori_loop(0, NCH, chunk, 0)

    def leave(src, dst):
        def pair(p, carry):
            o = src[pl.ds(pl.multiple_of(p * L, L), L), :]
            d = lax.dot_general(i_mat[...], o, NT, preferred_element_type=F32).astype(BF16)
            both = jnp.concatenate([d[: L // 2], d[L // 2 :]], axis=1)
            xs = jnp.dot(both, s_mat[...], preferred_element_type=F32)
            r0 = pl.multiple_of(p * 2 * R, 2 * R)
            t1[pl.ds(r0, R), :] = xs[:, :Z]
            t1[pl.ds(r0 + R, R), :] = xs[:, Z:]
            return carry

        lax.fori_loop(0, Y // 2, pair, 0)

        def channel(c, carry):
            for x in range(X):
                dst[c, x] = t1[pl.ds(x * C + c, Y, stride=X * C), :].astype(BF16)
            return carry

        lax.fori_loop(0, C, channel, 0)

    def flip(vo, vt):
        def pair(p, carry):
            rows = vo[pl.ds(row_of(2 * p + 1), 2 * R), :]
            wide = rows.astype(F32)
            for k in range(2):
                bs[k, 8 : 8 + R, :] = wide[k * R : (k + 1) * R]
            shifted = jnp.concatenate(
                [jnp.where(z0, bs[k, 9 : 9 + R, :], bs[k, 7 : 7 + R, :]) for k in range(2)], axis=0
            ).astype(BF16)
            cols = pl.ds(pl.multiple_of(p * 2 * R, 2 * R), 2 * R)
            for k, part in enumerate((rows, shifted)):
                vt[k * L : (k + 1) * L, cols] = lax.dot_general(
                    i_mat[...], part, NT, preferred_element_type=F32
                ).astype(BF16)
            return carry

        lax.fori_loop(0, Y // 2, pair, 0)

    half = CR // 2

    def pack(e, c, vs, center):
        for p in range(CH // 2):
            a, b = vs[2 * p], vs[2 * p + 1]
            rows = slice(p * (R + 16), p * (R + 16) + R)
            spr[e, c, rows, :] = jnp.where(xb, a, pltpu.roll(b, L - C, 1)).astype(BF16)
            spl[e, c, rows, :] = jnp.where(xb, pltpu.roll(b, C, 1), a).astype(BF16)
        if center is not None:
            center = center.astype(BF16)
            spr[e, c, R : R + 16, :] = center
            spl[e, c, R : R + 16, :] = center

        @pl.when(c == 0)
        def _():
            se[e, 0, 0:R, :] = vs[0].astype(BF16)
            if center is not None:
                se[e, 0, R : R + 16, :] = center

        @pl.when(c == NCH - 1)
        def _():
            se[e, 1, 0:R, :] = vs[CH - 1].astype(BF16)
            if center is not None:
                se[e, 1, R : R + 16, :] = center

    def copy_of(e, index, src, dst, dx, dy):
        return lambda: pltpu.make_async_remote_copy(
            src_ref=src, dst_ref=dst,
            send_sem=hs_sem.at[e, index], recv_sem=hr_sem.at[e, index],
            device_id=(lax.rem(gx + dx + nx, nx), lax.rem(gy + dy + ny, ny)),
            device_id_type=MESH,
        )

    def side_copies(e, c):
        return [
            (has_r, has_l, copy_of(e, c, spr.at[e, c], rl.at[e, c], 1, 0)),
            (has_l, has_r, copy_of(e, NCH + c, spl.at[e, c], rr.at[e, c], -1, 0)),
        ]

    def end_copies(e):
        low, high = pl.ds(0, R + 16), pl.ds(R, R + 16)
        both = jnp.logical_and
        m = 2 * NCH
        last = NCH - 1
        return [
            [
                (has_d, has_u, copy_of(e, m, se.at[e, 0], re.at[e, 1], 0, -1)),
                (both(has_r, has_d), both(has_l, has_u),
                 copy_of(e, m + 2, spr.at[e, 0, low], rdl.at[e, 1], 1, -1)),
                (both(has_l, has_d), both(has_r, has_u),
                 copy_of(e, m + 4, spl.at[e, 0, low], rdr.at[e, 1], -1, -1)),
            ],
            [
                (has_u, has_d, copy_of(e, m + 1, se.at[e, 1], re.at[e, 0], 0, 1)),
                (both(has_r, has_u), both(has_l, has_d),
                 copy_of(e, m + 3, spr.at[e, last, high], rdl.at[e, 0], 1, 1)),
                (both(has_l, has_u), both(has_r, has_d),
                 copy_of(e, m + 5, spl.at[e, last, high], rdr.at[e, 0], -1, 1)),
            ],
        ]

    def start(copies):
        for sends, _, copy in copies:
            @pl.when(sends)
            def _(copy=copy):
                copy().start()

    def arrive(copies):
        for _, takes, copy in copies:
            @pl.when(takes)
            def _(copy=copy):
                copy().wait_recv()

    def send(e, c):
        start(side_copies(e, c))

        @pl.when(c == 0)
        def _():
            start(end_copies(e)[0])

        @pl.when(c == NCH - 1)
        def _():
            start(end_copies(e)[1])

    def send_all(e):
        def body(c, carry):
            send(e, c)
            return carry

        lax.fori_loop(0, NCH, body, 0)

    def arrive_ends(e):
        for copies in end_copies(e):
            arrive(copies)

    def arrive_all(e):
        def body(c, carry):
            arrive(side_copies(e, c))
            return carry

        lax.fori_loop(0, NCH, body, 0)
        arrive_ends(e)

    def sent_all(e):
        def done(copies):
            for sends, _, copy in copies:
                @pl.when(sends)
                def _(copy=copy):
                    copy().wait_send()

        def body(c, carry):
            done(side_copies(e, c))
            return carry

        lax.fori_loop(0, NCH, body, 0)
        for copies in end_copies(e):
            done(copies)

    def center_of(tile):
        wide = tile.astype(F32)
        return (wide[0:8] + wide[8:16])[0:1]

    def halo_rows(e, c):
        center = jnp.where(xb, center_of(rl[e, c, R : R + 16, :]), center_of(rr[e, c, R : R + 16, :]))
        found = []
        for p in range(CH // 2):
            rows = slice(p * (R + 16), p * (R + 16) + R)
            a, b = rl[e, c, rows, :].astype(F32), rr[e, c, rows, :].astype(F32)
            found.append(jnp.where(xb, a, b))
            found.append(jnp.where(xb, pltpu.roll(a, C, 1), pltpu.roll(b, L - C, 1)))
        return found, center

    def end_rows(e, side):
        own, own_center = re[e, side, 0:R, :].astype(F32), center_of(re[e, side, R : R + 16, :])
        data, tile = (slice(16, 16 + R), slice(0, 16)) if side == 0 else (slice(0, R), slice(R, R + 16))
        a, b = rdl[e, side, data, :].astype(F32), rdr[e, side, data, :].astype(F32)
        center = jnp.where(xb, center_of(rdl[e, side, tile, :]), center_of(rdr[e, side, tile, :]))
        if side == 0:
            a, b = pltpu.roll(a, C, 1), pltpu.roll(b, L - C, 1)
        return own, own_center, jnp.where(xb, a, b), center

    END = (0, Y + 1)

    def each_halo(e, use_halo, use_own):
        def body(c, carry):
            found, center = halo_rows(e, c)
            for k, value in enumerate(found):
                use_halo(row_of(c * CH + k + 1), value, center, keep_h)
            return carry

        lax.fori_loop(0, NCH, body, 0)
        each_end(e, use_halo, use_own)

    def each_end(e, use_halo, use_own):
        for side in range(2):
            own, own_center, value, center = end_rows(e, side)
            use_own(END[side] * R, own, own_center, keep_o[side])
            use_halo(END[side] * R, value, center, keep_ho[side])

    def stats_copy(r, k):
        other = lax.rem(me + k, n)
        return pltpu.make_async_remote_copy(
            src_ref=msg.at[r], dst_ref=st.at[r, me],
            send_sem=ss_sem.at[r % 2, k], recv_sem=sr_sem.at[r % 2, me],
            device_id=coords(other), device_id_type=MESH,
        )

    def stats_send(r, top, low):
        row = lax.broadcasted_iota(jnp.int32, (2, L), 0)
        both = jnp.where(row == 0, top, low)
        msg[r] = both
        st[r, me] = both

        def body(k, carry):
            stats_copy(r, k).start()
            return carry

        lax.fori_loop(1, n, body, 0)

    def stats_wait(r):
        def body(k, carry):
            other = lax.rem(me + k, n)
            pltpu.make_async_remote_copy(
                src_ref=msg.at[r], dst_ref=st.at[r, other],
                send_sem=ss_sem.at[r % 2, k], recv_sem=sr_sem.at[r % 2, other],
                device_id=coords(other), device_id_type=MESH,
            ).wait()
            return carry

        lax.fori_loop(1, n, body, 0)
        return jnp.sum(st[r], axis=0)

    def piece_copy(w, phase, k, other, source):
        src = pk.at[w, other] if phase == 0 else ags.at[w]
        dst = (rsb if phase == 0 else agb).at[w, source]
        return pltpu.make_async_remote_copy(
            src_ref=src, dst_ref=dst,
            send_sem=ws_sem.at[w, phase, k], recv_sem=wr_sem.at[w, phase, source],
            device_id=coords(other), device_id_type=MESH,
        )

    def pieces_send(w, phase):
        def body(k, carry):
            piece_copy(w, phase, k, lax.rem(me + k, n), me).start()
            return carry

        lax.fori_loop(1, n, body, 0)

    def pieces_wait(w, phase):
        def body(k, carry):
            other = lax.rem(me + k, n)
            piece_copy(w, phase, k, other, other).wait()
            return carry

        lax.fori_loop(1, n, body, 0)

    def kernel_terms(w, vt, vo, vh):
        for j in range(3):
            g = jnp.concatenate([vo[j * R : (j + Y) * R, :], vh[j * R : (j + Y) * R, :]], axis=1)
            raw[j] = jnp.dot(vt[...], g, preferred_element_type=F32)
        block = lax.broadcasted_iota(jnp.int32, (C, L), 1) // C
        rows_v = cols_a + cols_b
        groups = [jnp.zeros((C, L), F32) for _ in range(7)]
        for j in range(3):
            dy = 2 - j
            for dx in range(3):
                for dz in range(3):
                    tap = dx * 9 + dy * 3 + dz
                    group, slot = tap // 4, tap % 4
                    for kb, (xv, zv) in enumerate(rows_v):
                        for cb, (xg, zg) in enumerate(rows_in):
                            if kb >= 4 and zv == 2 and zg != 1:
                                continue
                            if kb >= 4 and zv == -1 and zg != 0:
                                continue
                            if xv - xg + 1 != dx or zv - zg + 1 != dz:
                                continue
                            t, b = cb // 4, cb % 4
                            part = raw[j, kb * C : (kb + 1) * C, t * L : (t + 1) * L]
                            if slot != b:
                                part = pltpu.roll(part, (slot - b) % 4 * C, 1)
                            groups[group] = groups[group] + jnp.where(block == slot, part, 0.0)
        flat = jnp.concatenate(groups, axis=0)
        rows = n * PIECE
        if rows > flat.shape[0]:
            flat = jnp.concatenate([flat, jnp.zeros((rows - flat.shape[0], L), F32)], axis=0)
        pk[w] = flat.reshape(n, PIECE, L)
        rsb[w, me] = pk[w, me]
        pieces_send(w, 0)

    def pieces_sum(w):
        pieces_wait(w, 0)
        whole = jnp.sum(rsb[w], axis=0)
        ags[w] = whole
        agb[w, me] = whole
        pieces_send(w, 1)

    def pieces_out(w, out_ref, scale):
        pieces_wait(w, 1)
        flat = agb[w].reshape(n * PIECE, L)
        for group in range(7):
            tall = jnp.transpose(flat[group * C : (group + 1) * C]) * scale
            for slot in range(4):
                tap = 4 * group + slot
                if tap < 27:
                    out_ref[tap] = tall[slot * C : (slot + 1) * C]

    def conv_rows(vo, vh, w_ref, c):
        parts = []
        for j in range(3):
            rows = pl.ds(row_of(c * CH + j), CR)
            parts += [vo[rows, :], vh[rows, :]]
        ab = jnp.dot(
            jnp.concatenate(parts, axis=1), w_ref[...].reshape(6 * L, 2 * L),
            preferred_element_type=F32,
        )
        for k in range(CH):
            bs[k, 8 : 8 + R, :] = ab[k * R : (k + 1) * R, L:]
        return [
            ab[k * R : (k + 1) * R, :L]
            + jnp.where(z0, bs[k, 7 : 7 + R, :], bs[k, 9 : 9 + R, :])
            for k in range(CH)
        ]

    def centered(vs):
        s = fold(one(functools.reduce(jnp.add, [eight(v) for v in vs])))
        mean = s / (4.0 * CR)
        high = mean.astype(BF16).astype(F32)
        low = (mean - high).astype(BF16).astype(F32)
        tile = jnp.concatenate(
            [jnp.broadcast_to(high, (8, L)), jnp.broadcast_to(low, (8, L))], axis=0
        )
        return s, high + low, tile

    cells = float(X * Y * Z)
    zero8 = jnp.zeros((8, L), F32)

    def forward_loop(vo, vh, w_ref, hc, centers, e, before):
        def body(c, squares):
            before(c)
            hs = conv_rows(vo, vh, w_ref, c)
            s, center, tile = centered(hs)
            centers[pl.ds(c, 1), :] = center
            scs[pl.ds(c, 1), :] = s
            hs = [h - center for h in hs]
            for k in range(CH):
                hc[pl.ds(row_of(c * CH + k), R), :] = hs[k]
                squares = squares + eight(hs[k] * hs[k])
            pack(e, c, hs, tile)
            send(e, c)
            return squares

        squares = fold(one(lax.fori_loop(0, NCH, body, zero8)))
        mean = one(scs[...]) / cells
        off = centers[...] - mean
        rest = scs[...] - (4.0 * CR) * centers[...]
        spread = squares + one(off * (2.0 * rest + (4.0 * CR) * off))
        return mean, spread

    def moments(r):
        sums = stats_wait(r)
        center = sums[0:1] / n

        def body(d, acc):
            off = st[r, d] - center
            return acc + off * off

        between = lax.fori_loop(0, n, body, jnp.zeros((2, L), F32))[0:1]
        variance = (sums[1:2] + cells * between) / total
        return center, lax.rsqrt(variance + EPSILON)

    build(k1_ref, wf1, True)
    enter(f_ref, vo_f, FEAT)
    pl.semaphore_wait(barrier, n - 1)
    send_all(FEAT)
    build(k2_ref, wf2, True)
    enter(c_ref, vo_c, COT)
    flip(vo_f, vt_f)

    def put_f(dst):
        def use(row, value, center, keep):
            dst[pl.ds(row, R), :] = jnp.where(keep, value, 0.0).astype(BF16)

        return use

    arrive_ends(FEAT)
    each_end(FEAT, put_f(vh_f), put_f(vo_f))

    def take_f(c):
        arrive(side_copies(FEAT, c))
        found, _ = halo_rows(FEAT, c)
        for k, value in enumerate(found):
            put_f(vh_f)(row_of(c * CH + k + 1), value, None, keep_h)

    take_f(0)

    def before_f(c):
        @pl.when(c < NCH - 1)
        def _():
            take_f(c + 1)

    mean, spread = forward_loop(vo_f, vh_f, wf1, hc1, mcs1, HID1, before_f)
    stats_send(0, mean, spread)
    build(k2_ref, wb2, False)
    build(k1_ref, wb1, False)
    center, inv1 = moments(0)
    arrive_all(HID1)
    send_all(COT)

    def put_a(n_dst, v_dst, inv, gain, bias, center):
        def use(row, value, mid, keep):
            normed = (value + (mid - center)) * inv
            n_dst[pl.ds(row, R), :] = normed
            a = activate(normed * gain + bias)
            v_dst[pl.ds(row, R), :] = (a if keep is None else jnp.where(keep, a, 0.0)).astype(BF16)

        return use

    own_a = put_a(n1o, vo_a, inv1, gain1, bias1, center)

    def own_active(c, carry):
        mid = mcs1[pl.ds(c, 1), :]
        for k in range(CH):
            own_a(row_of(c * CH + k + 1), hc1[pl.ds(row_of(c * CH + k), R), :], mid, None)
        return carry

    lax.fori_loop(0, NCH, own_active, 0)
    each_halo(HID1, put_a(n1h, vh_a, inv1, gain1, bias1, center), own_a)

    mean, spread = forward_loop(vo_a, vh_a, wf2, hc2, mcs, HID2, lambda c: None)
    stats_send(1, mean, spread)
    flip(vo_a, vt_a)
    center, inv2 = moments(1)

    def own_output(c, carry):
        plain, along = carry
        mid = mcs[pl.ds(c, 1), :]
        for k in range(CH):
            y = c * CH + k
            normed = (hc2[pl.ds(row_of(y), R), :] + (mid - center)) * inv2
            shifted = normed * gain2 + bias2
            outb[pl.ds(row_of(y), R), :] = activate(shifted).astype(BF16)
            rows = pl.ds(row_of(y + 1), R)
            slope = vo_c[rows, :].astype(F32) * activate_slope(shifted)
            n2o[rows, :] = normed
            s2o[rows, :] = slope
            plain = plain + eight(slope)
            along = along + eight(slope * normed)
        return plain, along

    plain, along = lax.fori_loop(0, NCH, own_output, (zero8, zero8))
    stats_send(2, fold(one(plain)), fold(one(along)))

    arrive_all(COT)
    arrive_all(HID2)

    def put_c(dst):
        def use(row, value, mid, keep):
            dst[pl.ds(row, R), :] = value.astype(BF16)

        return use

    each_halo(COT, put_c(vh_c), put_c(vo_c))

    def put_s(n_dst, s_dst, c_src):
        def use(row, value, mid, keep):
            rows = pl.ds(row, R)
            normed = (value + (mid - center)) * inv2
            n_dst[rows, :] = normed
            s_dst[rows, :] = c_src[rows, :].astype(F32) * activate_slope(normed * gain2 + bias2)

        return use

    each_halo(HID2, put_s(n2h, s2h, vh_c), put_s(n2o, s2o, vo_c))
    leave(outb, o_ref)
    sums2 = stats_wait(2)

    def gradient(slope, normed, sums, factor):
        return factor * (slope - sums[0:1] / total - normed * (sums[1:2] / total))

    factor2 = gain2 * inv2

    def grad_rows(row, keep_own, keep_halo):
        rows = pl.ds(row, R)
        g = gradient(s2o[rows, :], n2o[rows, :], sums2, factor2)
        vo_g[rows, :] = (g if keep_own is None else jnp.where(keep_own, g, 0.0)).astype(BF16)
        g = gradient(s2h[rows, :], n2h[rows, :], sums2, factor2)
        vh_g[rows, :] = jnp.where(keep_halo, g, 0.0).astype(BF16)

    def grad_two(c, carry):
        for k in range(CH):
            grad_rows(row_of(c * CH + k + 1), None, keep_h)
        return carry

    lax.fori_loop(0, NCH, grad_two, 0)
    for side in range(2):
        grad_rows(END[side] * R, keep_o[side], keep_ho[side])

    def back_loop(c, carry):
        plain, along = carry
        slopes = []
        for k, back in enumerate(conv_rows(vo_g, vh_g, wb2, c)):
            rows = pl.ds(row_of(c * CH + k + 1), R)
            normed = n1o[rows, :]
            slope = back * activate_slope(normed * gain1 + bias1)
            s1o[rows, :] = slope
            plain = plain + eight(slope)
            along = along + eight(slope * normed)
            slopes.append(slope)
        _, mid, tile = centered(slopes)
        pack(SLO1, c, [v - mid for v in slopes], tile)
        send(SLO1, c)
        return plain, along

    plain, along = lax.fori_loop(0, NCH, back_loop, (zero8, zero8))
    stats_send(3, fold(one(plain)), fold(one(along)))
    kernel_terms(1, vt_a, vo_g, vh_g)
    sums1 = stats_wait(3)
    arrive_all(SLO1)
    factor1 = gain1 * inv1

    def put_g(dst, normed_ref):
        def use(row, value, mid, keep):
            rows = pl.ds(row, R)
            g = gradient(value + mid, normed_ref[rows, :], sums1, factor1)
            dst[rows, :] = jnp.where(keep, g, 0.0).astype(BF16)

        return use

    def grad_one(c, carry):
        for k in range(CH):
            rows = pl.ds(row_of(c * CH + k + 1), R)
            vo_g[rows, :] = gradient(s1o[rows, :], n1o[rows, :], sums1, factor1).astype(BF16)
        return carry

    lax.fori_loop(0, NCH, grad_one, 0)
    each_halo(SLO1, put_g(vh_g, n1h), put_g(vo_g, n1o))
    kernel_terms(0, vt_f, vo_g, vh_g)
    pieces_sum(1)

    def last_loop(c, carry):
        for k, back in enumerate(conv_rows(vo_g, vh_g, wb1, c)):
            outb[pl.ds(row_of(c * CH + k), R), :] = back.astype(BF16)
        return carry

    lax.fori_loop(0, NCH, last_loop, 0)
    pieces_sum(0)
    leave(outb, fg_ref)
    scale = 1.0 / (total ** 0.5)
    for row, (sums, part) in enumerate(((sums1, 1), (sums1, 0), (sums2, 1), (sums2, 0))):
        ng_ref[row : row + 1, :] = sums[part : part + 1, 0:C] * scale
    pieces_out(1, dk2_ref, scale)
    pieces_out(0, dk1_ref, scale)
    for e in range(NEXCH):
        sent_all(e)


def local(features, kernel_one, gain_one, bias_one, kernel_two, gain_two, bias_two, cotangent):
    C, X, Y, Z = features.shape
    nx, ny = lax.axis_size("gx"), lax.axis_size("gy")
    n = nx * ny
    total = float(X * Y * Z * nx * ny)
    R = Z // 2
    NCH = Y // CH
    piece = -(-224 // (8 * n)) * 8
    taps = lambda k: jnp.transpose(k, (2, 3, 4, 0, 1)).reshape(27, C, C)
    row = lambda v: v.reshape(1, C)
    rows, all_rows = Y * R, (Y + 2) * R
    packed = CH * R // 2 + 16
    V = pltpu.VMEM
    DMA = pltpu.SemaphoreType.DMA
    scratch = [
        V((rows, L), F32), V((8, L), F32), V((R, 2 * Z), BF16), V((2 * L, 2 * Z), BF16),
        V((L, L), BF16), V((27, C, L), F32),
    ]
    scratch += [V((3, 2 * L, 2 * L), BF16)] * 4
    scratch += [V((all_rows, L), BF16)] * 8
    scratch += [V((2 * L, rows), BF16)] * 2
    scratch += [V((rows, L), F32)] * 2
    scratch += [V((all_rows, L), F32)] * 7
    scratch += [
        V((rows, L), BF16), V((CH, R + 16, L), F32), V((NCH, L), F32), V((NCH, L), F32),
        V((NCH, L), F32), V((3, 2 * L, 2 * L), F32),
    ]
    scratch += [V((NEXCH, NCH, packed, L), BF16)] * 2 + [V((NEXCH, 2, R + 16, L), BF16)]
    scratch += [V((NEXCH, NCH, packed, L), BF16)] * 2 + [V((NEXCH, 2, R + 16, L), BF16)] * 3
    scratch += [DMA((NEXCH, 2 * NCH + 6))] * 2
    scratch += [V((4, 2, L), F32), V((4, n, 2, L), F32), DMA((2, n)), DMA((2, n))]
    scratch += [
        V((2, n, piece, L), F32), V((2, n, piece, L), F32), V((2, piece, L), F32),
        V((2, n, piece, L), F32), DMA((2, 2, n)), DMA((2, 2, n)),
    ]
    vmem = pl.BlockSpec(memory_space=pltpu.VMEM)
    out, fg, dk1, dk2, norm = pl.pallas_call(
        functools.partial(kernel, nx, ny, total),
        name="blocks",
        out_shape=[
            jax.ShapeDtypeStruct((C, X, Y, Z), BF16), jax.ShapeDtypeStruct((C, X, Y, Z), BF16),
            jax.ShapeDtypeStruct((27, C, C), F32), jax.ShapeDtypeStruct((27, C, C), F32),
            jax.ShapeDtypeStruct((4, C), F32),
        ],
        in_specs=[vmem] * 8,
        out_specs=[vmem] * 5,
        scratch_shapes=scratch,
        compiler_params=pltpu.CompilerParams(
            collective_id=0, has_side_effects=True, vmem_limit_bytes=62 << 20
        ),
    )(
        features, cotangent, taps(kernel_one), taps(kernel_two),
        row(gain_one), row(bias_one), row(gain_two), row(bias_two),
    )
    untap = lambda d: jnp.transpose(d.reshape(3, 3, 3, C, C), (3, 4, 0, 1, 2))
    return out, fg, untap(dk1), untap(dk2), norm


def solution(mesh):
    in_specs = (P(None, "gx", "gy", None), P(), P(), P(), P(), P(), P(), P(None, "gx", "gy", None))
    out_specs = (P(None, "gx", "gy", None), P(None, "gx", "gy", None), P(), P(), P())
    return jax.shard_map(local, mesh=mesh, in_specs=in_specs, out_specs=out_specs, check_vma=False)
```

time: 155 us -> 96.3 us (0.62)
  Pallas kernels: 137 us -> 89.7 us
  local copies, waits for them, and re-layouts: 16.3 us -> 5.65 us
    pallas_call x13 -> x1, Pallas kernels: 137 us -> 89.7 us  [local(): pl.pallas_call(functools.partial(kernel, nx, ny, total), name='blocks', o...]
    reshape x4 -> x0, local copies, waits for them, and re-layouts: 3.21 us -> none  [the longest x2 1.61 us: behind(): return jnp.transpose(kernel, (2, 3, 1, 4, 0)).reshape(9 * C, 3 * C)]
    unnamed x24 -> x13, local copies, waits for them, and re-layouts: 8.74 us -> 5.65 us
    slice x2 -> x0, local copies, waits for them, and re-layouts: 1.77 us -> none  [the longest x1 1 us: local(): summed[9 * C:]]
where the time goes in v1:
time: 96.3 us; the launch traced here: 96 us
  Pallas kernels  89.7 us (93%)
  local copies, waits for them, and re-layouts  5.65 us (6%)
    pallas_call x1, Pallas kernels, local(): pl.pallas_call(functools.partial(kernel, nx, ny, total), name='blocks', o...  89.7 us
    unnamed x13, local copies, waits for them, and re-layouts  5.65 us

profile of v1, /device:TPU:0, one launch (start us, length us, event | category | flops | bytes accessed | tf_op | source)
XLA Modules:
  0.0 96.0 jit_solution(9319723629528497013)
XLA Ops:
  0.6 89.7 %blocks.1 = (bf16[32,2,32,128]{3,2,1,0:T(8,128)(2,1)}, bf16[32,2,32,128]{3,2,1,0:T(8,128)(2,1)}, f32[27,32,32]{2,1,0:T(8,128)}, f32[27,32,32]{2,1,0:T(8,128)}, f32[4,32]{1,0:T(4,128)}) custom-call(bf16[32,2,32,128]{3,2,1,0:T(8,128)(2,1)} %f_ref.1, bf16[32,2,32,128]{3,2,1,0:T(8,128)(2,1)} %c_ref.1, bf16[27,32,32]{2,1,0:T(8,128)(2,1)} %bitcast.18, ...), custom_call_target="tpu_custom_call" | custom-call | tf_op jit(solution)/shard_map/blocks/pallas_call | solution.py:773
  90.3 0.0 copy-start
  90.3 1.9 %copy.18 = bf16[32,2,32,128]{3,2,1,0:T(8,128)(2,1)} copy(bf16[32,2,32,128]{3,2,1,0:T(8,128)(2,1)} %get-tuple-element.20) | data formatting | bytes 1048576
  92.3 0.0 copy-done
  92.3 0.0 copy-start.2
  92.3 0.8 copy.19
  93.1 0.4 copy-done.2
  93.5 0.0 copy-start.1
  93.5 0.8 copy.20
  94.2 0.4 copy-done.1
  94.7 0.0 copy-start.3
  94.7 0.8 copy.21
  95.4 0.0 copy-done.3
  95.4 0.6 copy.22
Async XLA Ops:
  90.3 1.9 %copy-start = (bf16[32,2,32,128]{3,2,1,0:T(8,128)(2,1)S(1)}, bf16[32,2,32,128]{3,2,1,0:T(8,128)(2,1)}, u32[]{:S(2)}) copy-start(bf16[32,2,32,128]{3,2,1,0:T(8,128)(2,1)} %get-tuple-element.21) | copy-start | bytes 1572868
  92.3 1.2 %copy-start.2 = (f32[27,32,32]{2,1,0:T(8,128)S(1)}, f32[27,32,32]{2,1,0:T(8,128)}, u32[]{:S(2)}) copy-start(f32[27,32,32]{2,1,0:T(8,128)} %get-tuple-element.12) | copy-start | bytes 331780
  93.5 1.2 %copy-start.1 = (f32[27,32,32]{2,1,0:T(8,128)S(1)}, f32[27,32,32]{2,1,0:T(8,128)}, u32[]{:S(2)}) copy-start(f32[27,32,32]{2,1,0:T(8,128)} %get-tuple-element.13) | copy-start | bytes 331780
  94.7 0.8 copy-start.3

commit v2 on v1

--- a/solution.py
+++ b/solution.py
@@ -11,6 +11,7 @@
 SLOPE = 0.01
 SHARPNESS = 8.0
 MESH = pl.DeviceIdType.MESH
+LOGICAL = pl.DeviceIdType.LOGICAL
 F32 = jnp.float32
 BF16 = jnp.bfloat16
 L = 128
@@ -33,14 +34,15 @@
 
 def kernel(
     nx, ny, total,
-    f_ref, c_ref, k1_ref, k2_ref, g1_ref, b1_ref, g2_ref, b2_ref,
-    o_ref, fg_ref, dk1_ref, dk2_ref, ng_ref,
+    f_hbm, c_hbm, k1_hbm, k2_hbm, g1_hbm, b1_hbm, g2_hbm, b2_hbm,
+    o_ref, fg_ref, dk_ref, ng_ref,
     t1, par, e_mat, s_mat, i_mat, base, wf1, wf2, wb2, wb1,
     vo_f, vh_f, vo_c, vh_c, vo_a, vh_a, vo_g, vh_g, vt_f, vt_a,
     hc1, hc2, n1o, n1h, n2o, n2h, s2o, s2h, s1o, outb, bs, mcs, scs, mcs1, raw,
     spr, spl, se, rl, rr, re, rdl, rdr, hs_sem, hr_sem,
     msg, st, ss_sem, sr_sem,
     pk, rsb, ags, agb, ws_sem, wr_sem,
+    f_ref, c_ref, k1_ref, k2_ref, g1_ref, b1_ref, g2_ref, b2_ref, in_sem, rel, rel_sem, fwd_sem,
 ):
     C, X, Y, Z = f_ref.shape
     R = Z // 2
@@ -53,15 +55,26 @@
     has_l, has_r = gx > 0, gx < nx - 1
     has_d, has_u = gy > 0, gy < ny - 1
 
-    def coords(d):
-        return (d // ny, lax.rem(d, ny))
+    def peer(k):
+        other = me + k
+        return jnp.where(other >= n, other - n, other)
+
+    fetch = [
+        pltpu.make_async_copy(src, dst, in_sem.at[k])
+        for k, (src, dst) in enumerate(
+            (
+                (k1_hbm, k1_ref), (f_hbm, f_ref), (k2_hbm, k2_ref), (c_hbm, c_ref),
+                (g1_hbm, g1_ref), (b1_hbm, b1_ref), (g2_hbm, g2_ref), (b2_hbm, b2_ref),
+            )
+        )
+    ]
+    for copy in fetch:
+        copy.start()
 
     barrier = pltpu.get_barrier_semaphore()
 
     def hello(k, carry):
-        pl.semaphore_signal(
-            barrier, inc=1, device_id=coords(lax.rem(me + k, n)), device_id_type=MESH
-        )
+        pl.semaphore_signal(barrier, inc=1, device_id=peer(k), device_id_type=LOGICAL)
         return carry
 
     lax.fori_loop(1, n, hello, 0)
@@ -81,6 +94,14 @@
     def fold(v):
         v = v + pltpu.roll(v, C, 1)
         return v + pltpu.roll(v, 2 * C, 1)
+
+    def loop(count, body, carry=0, unroll=1):
+        def group(i, carry):
+            for k in range(unroll):
+                carry = body(i * unroll + k, carry)
+            return carry
+
+        return lax.fori_loop(0, count // unroll, group, carry)
 
     def eight(v):
         return jnp.sum(v.reshape(v.shape[0] // 8, 8, L), axis=0)
@@ -102,11 +123,6 @@
     r_i = lax.broadcasted_iota(jnp.int32, (L, L), 0)
     c_i = lax.broadcasted_iota(jnp.int32, (L, L), 1)
     i_mat[...] = jnp.where(r_i == c_i, 1.0, 0.0).astype(BF16)
-    par[...] = jnp.zeros(par.shape, F32)
-    for row, ref in enumerate((g1_ref, b1_ref, g2_ref, b2_ref)):
-        par[row : row + 1, 0:C] = ref[...]
-    params = fold(par[...])
-    gain1, bias1, gain2, bias2 = [params[r : r + 1] for r in range(4)]
     bs[...] = jnp.zeros(bs.shape, F32)
 
     spots_in = [(0, 0, z, x) for z in range(2) for x in range(2)]
@@ -157,7 +173,7 @@
             )
             return carry
 
-        lax.fori_loop(0, C, widen, 0)
+        loop(C, widen, unroll=4)
         zero = jnp.zeros((X * C, Z), BF16)
 
         def chunk(c, carry):
@@ -177,7 +193,7 @@
             pack(e, c, vs, None)
             return carry
 
-        lax.fori_loop(0, NCH, chunk, 0)
+        loop(NCH, chunk, unroll=2)
 
     def leave(src, dst):
         def pair(p, carry):
@@ -190,23 +206,27 @@
             t1[pl.ds(r0 + R, R), :] = xs[:, Z:]
             return carry
 
-        lax.fori_loop(0, Y // 2, pair, 0)
+        with jax.named_scope("leave_pairs"):
+            loop(Y // 2, pair, unroll=4)
 
         def channel(c, carry):
             for x in range(X):
                 dst[c, x] = t1[pl.ds(x * C + c, Y, stride=X * C), :].astype(BF16)
             return carry
 
-        lax.fori_loop(0, C, channel, 0)
+        with jax.named_scope("leave_channels"):
+            loop(C, channel, unroll=4)
 
     def flip(vo, vt):
         def pair(p, carry):
             rows = vo[pl.ds(row_of(2 * p + 1), 2 * R), :]
             wide = rows.astype(F32)
+            slot = 2 * lax.rem(p, 4)
             for k in range(2):
-                bs[k, 8 : 8 + R, :] = wide[k * R : (k + 1) * R]
+                bs[slot + k, 8 : 8 + R, :] = wide[k * R : (k + 1) * R]
             shifted = jnp.concatenate(
-                [jnp.where(z0, bs[k, 9 : 9 + R, :], bs[k, 7 : 7 + R, :]) for k in range(2)], axis=0
+                [jnp.where(z0, bs[slot + k, 9 : 9 + R, :], bs[slot + k, 7 : 7 + R, :]) for k in range(2)],
+                axis=0,
             ).astype(BF16)
             cols = pl.ds(pl.multiple_of(p * 2 * R, 2 * R), 2 * R)
             for k, part in enumerate((rows, shifted)):
@@ -215,7 +235,7 @@
                 ).astype(BF16)
             return carry
 
-        lax.fori_loop(0, Y // 2, pair, 0)
+        loop(Y // 2, pair, unroll=4)
 
     half = CR // 2
 
@@ -230,17 +250,14 @@
             spr[e, c, R : R + 16, :] = center
             spl[e, c, R : R + 16, :] = center
 
-        @pl.when(c == 0)
-        def _():
-            se[e, 0, 0:R, :] = vs[0].astype(BF16)
-            if center is not None:
-                se[e, 0, R : R + 16, :] = center
-
-        @pl.when(c == NCH - 1)
-        def _():
-            se[e, 1, 0:R, :] = vs[CH - 1].astype(BF16)
-            if center is not None:
-                se[e, 1, R : R + 16, :] = center
+        first = jnp.where(c == 0, 0, 2)
+        se[e, first, 0:R, :] = vs[0].astype(BF16)
+        if center is not None:
+            se[e, first, R : R + 16, :] = center
+        last = jnp.where(c == NCH - 1, 1, 2)
+        se[e, last, 0:R, :] = vs[CH - 1].astype(BF16)
+        if center is not None:
+            se[e, last, R : R + 16, :] = center
 
     def copy_of(e, index, src, dst, dx, dy):
         return lambda: pltpu.make_async_remote_copy(
@@ -290,23 +307,75 @@
             def _(copy=copy):
                 copy().wait_recv()
 
-    def send(e, c):
-        start(side_copies(e, c))
-
-        @pl.when(c == 0)
-        def _():
-            start(end_copies(e)[0])
-
-        @pl.when(c == NCH - 1)
-        def _():
-            start(end_copies(e)[1])
+    RELAY = nx == 8
+    ODD = range(NCH // 2)
+    low_mid, high_mid = nx // 2 - 1, nx // 2
+
+    def hop(e, h, src, dst, there, s_sem, r_sem):
+        return pltpu.make_async_remote_copy(
+            src_ref=src, dst_ref=dst, send_sem=s_sem, recv_sem=r_sem,
+            device_id=(there, gy), device_id_type=MESH,
+        )
+
+    def send_odd(e, c):
+        h = c // 2
+        (_, _, right), (_, _, left) = side_copies(e, c)
+        relays = (
+            (gx == low_mid, has_r, right, spr, nx - 1, hs_sem.at[e, c]),
+            (gx == high_mid, has_l, left, spl, 0, hs_sem.at[e, NCH + c]),
+        )
+        for via, sends, direct, src, there, s_sem in relays:
+            @pl.when(via)
+            def _(src=src, there=there, s_sem=s_sem):
+                hop(e, h, src.at[e, c], rel.at[e, h], there, s_sem, rel_sem.at[e, h]).start()
+
+            @pl.when(jnp.logical_and(sends, jnp.logical_not(via)))
+            def _(direct=direct):
+                direct().start()
+
+    def forwards(e, h):
+        c = 2 * h + 1
+        return (
+            (gx == nx - 1, hop(e, h, rel.at[e, h], rl.at[e, c], high_mid, fwd_sem.at[e, h], hr_sem.at[e, c])),
+            (gx == 0, hop(e, h, rel.at[e, h], rr.at[e, c], low_mid, fwd_sem.at[e, h], hr_sem.at[e, NCH + c])),
+        ) if RELAY else ()
+
+    def relay_arrives(e, h):
+        hop(e, h, rel.at[e, h], rel.at[e, h], low_mid, fwd_sem.at[e, h], rel_sem.at[e, h]).wait_recv()
+
+    def forward(e, which):
+        for h in which:
+            for here, copy in forwards(e, h):
+                @pl.when(here)
+                def _(h=h, copy=copy):
+                    relay_arrives(e, h)
+                    copy.start()
+
+    def forwarded(e):
+        for h in ODD:
+            for here, copy in forwards(e, h):
+                @pl.when(here)
+                def _(copy=copy):
+                    copy.wait_send()
+
+    def send(e, c, odd):
+        if RELAY and odd:
+            send_odd(e, c)
+        else:
+            start(side_copies(e, c))
+
+    def send_ends(e):
+        for copies in end_copies(e):
+            start(copies)
 
     def send_all(e):
-        def body(c, carry):
-            send(e, c)
-            return carry
-
-        lax.fori_loop(0, NCH, body, 0)
+        def body(h, carry):
+            send(e, 2 * h, False)
+            send(e, 2 * h + 1, True)
+            return carry
+
+        lax.fori_loop(0, NCH // 2, body, 0)
+        send_ends(e)
 
     def arrive_ends(e):
         for copies in end_copies(e):
@@ -376,14 +445,6 @@
             use_own(END[side] * R, own, own_center, keep_o[side])
             use_halo(END[side] * R, value, center, keep_ho[side])
 
-    def stats_copy(r, k):
-        other = lax.rem(me + k, n)
-        return pltpu.make_async_remote_copy(
-            src_ref=msg.at[r], dst_ref=st.at[r, me],
-            send_sem=ss_sem.at[r % 2, k], recv_sem=sr_sem.at[r % 2, me],
-            device_id=coords(other), device_id_type=MESH,
-        )
-
     def stats_send(r, top, low):
         row = lax.broadcasted_iota(jnp.int32, (2, L), 0)
         both = jnp.where(row == 0, top, low)
@@ -391,47 +452,43 @@
         st[r, me] = both
 
         def body(k, carry):
-            stats_copy(r, k).start()
+            pltpu.make_async_remote_copy(
+                src_ref=msg.at[r], dst_ref=st.at[r, me],
+                send_sem=ss_sem.at[r], recv_sem=sr_sem.at[r],
+                device_id=peer(k), device_id_type=LOGICAL,
+            ).start()
             return carry
 
         lax.fori_loop(1, n, body, 0)
 
     def stats_wait(r):
-        def body(k, carry):
-            other = lax.rem(me + k, n)
-            pltpu.make_async_remote_copy(
-                src_ref=msg.at[r], dst_ref=st.at[r, other],
-                send_sem=ss_sem.at[r % 2, k], recv_sem=sr_sem.at[r % 2, other],
-                device_id=coords(other), device_id_type=MESH,
-            ).wait()
-            return carry
-
-        lax.fori_loop(1, n, body, 0)
+        others = st.at[r, pl.ds(0, n - 1)]
+        pltpu.make_async_remote_copy(
+            src_ref=others, dst_ref=others, send_sem=ss_sem.at[r], recv_sem=sr_sem.at[r],
+            device_id=peer(1), device_id_type=LOGICAL,
+        ).wait()
         return jnp.sum(st[r], axis=0)
-
-    def piece_copy(w, phase, k, other, source):
-        src = pk.at[w, other] if phase == 0 else ags.at[w]
-        dst = (rsb if phase == 0 else agb).at[w, source]
-        return pltpu.make_async_remote_copy(
-            src_ref=src, dst_ref=dst,
-            send_sem=ws_sem.at[w, phase, k], recv_sem=wr_sem.at[w, phase, source],
-            device_id=coords(other), device_id_type=MESH,
-        )
 
     def pieces_send(w, phase):
         def body(k, carry):
-            piece_copy(w, phase, k, lax.rem(me + k, n), me).start()
+            other = peer(k)
+            pltpu.make_async_remote_copy(
+                src_ref=pk.at[w, other] if phase == 0 else ags.at[w],
+                dst_ref=(rsb if phase == 0 else agb).at[w, me],
+                send_sem=ws_sem.at[w, phase], recv_sem=wr_sem.at[w, phase],
+                device_id=other, device_id_type=LOGICAL,
+            ).start()
             return carry
 
         lax.fori_loop(1, n, body, 0)
 
     def pieces_wait(w, phase):
-        def body(k, carry):
-            other = lax.rem(me + k, n)
-            piece_copy(w, phase, k, other, other).wait()
-            return carry
-
-        lax.fori_loop(1, n, body, 0)
+        others = (rsb if phase == 0 else agb).at[w, pl.ds(0, n - 1)]
+        pltpu.make_async_remote_copy(
+            src_ref=others, dst_ref=others,
+            send_sem=ws_sem.at[w, phase], recv_sem=wr_sem.at[w, phase],
+            device_id=peer(1), device_id_type=LOGICAL,
+        ).wait()
 
     def kernel_terms(w, vt, vo, vh):
         for j in range(3):
@@ -469,22 +526,16 @@
 
     def pieces_sum(w):
         pieces_wait(w, 0)
-        whole = jnp.sum(rsb[w], axis=0)
+        whole = jnp.sum(rsb[w], axis=0).astype(BF16)
         ags[w] = whole
         agb[w, me] = whole
         pieces_send(w, 1)
 
-    def pieces_out(w, out_ref, scale):
+    def pieces_out(w):
         pieces_wait(w, 1)
-        flat = agb[w].reshape(n * PIECE, L)
-        for group in range(7):
-            tall = jnp.transpose(flat[group * C : (group + 1) * C]) * scale
-            for slot in range(4):
-                tap = 4 * group + slot
-                if tap < 27:
-                    out_ref[tap] = tall[slot * C : (slot + 1) * C]
-
-    def conv_rows(vo, vh, w_ref, c):
+        dk_ref[w] = agb[w].reshape(n * PIECE, L)
+
+    def conv_rows(vo, vh, w_ref, c, slot=0):
         parts = []
         for j in range(3):
             rows = pl.ds(row_of(c * CH + j), CR)
@@ -494,45 +545,76 @@
             preferred_element_type=F32,
         )
         for k in range(CH):
-            bs[k, 8 : 8 + R, :] = ab[k * R : (k + 1) * R, L:]
+            bs[slot + k, 8 : 8 + R, :] = ab[k * R : (k + 1) * R, L:]
         return [
             ab[k * R : (k + 1) * R, :L]
-            + jnp.where(z0, bs[k, 7 : 7 + R, :], bs[k, 9 : 9 + R, :])
+            + jnp.where(z0, bs[slot + k, 7 : 7 + R, :], bs[slot + k, 9 : 9 + R, :])
             for k in range(CH)
         ]
 
-    def centered(vs):
-        s = fold(one(functools.reduce(jnp.add, [eight(v) for v in vs])))
+    def totals(vs):
+        return fold(one(functools.reduce(jnp.add, [eight(v) for v in vs])))
+
+    def center_near(s):
         mean = s / (4.0 * CR)
         high = mean.astype(BF16).astype(F32)
         low = (mean - high).astype(BF16).astype(F32)
         tile = jnp.concatenate(
             [jnp.broadcast_to(high, (8, L)), jnp.broadcast_to(low, (8, L))], axis=0
         )
-        return s, high + low, tile
+        return high + low, tile
 
     cells = float(X * Y * Z)
     zero8 = jnp.zeros((8, L), F32)
-
-    def forward_loop(vo, vh, w_ref, hc, centers, e, before):
-        def body(c, squares):
-            before(c)
-            hs = conv_rows(vo, vh, w_ref, c)
-            s, center, tile = centered(hs)
-            centers[pl.ds(c, 1), :] = center
-            scs[pl.ds(c, 1), :] = s
-            hs = [h - center for h in hs]
-            for k in range(CH):
-                hc[pl.ds(row_of(c * CH + k), R), :] = hs[k]
-                squares = squares + eight(hs[k] * hs[k])
-            pack(e, c, hs, tile)
-            send(e, c)
-            return squares
-
-        squares = fold(one(lax.fori_loop(0, NCH, body, zero8)))
+    PAIR = 2
+
+    def paired(e, step, carry, before=None):
+        def group(i, carry, first):
+            inner, s = carry
+            if before is not None:
+                before(i)
+            found = []
+            for k in range(PAIR):
+                inner, vs = step(i * PAIR + k, k * CH, inner)
+                found.append((vs, totals(vs)))
+            center, tile = center_near(found[0][1] if first else s)
+            for k, (vs, s) in enumerate(found):
+                c = i * PAIR + k
+                centers_of[e][pl.ds(c, 1), :] = center
+                scs[pl.ds(c, 1), :] = s
+                inner = keep_chunk(e, c, vs, center, tile, inner)
+            if e != HID2:
+                for k in range(PAIR):
+                    send(e, i * PAIR + k, k % 2 == 1)
+            return inner, s
+
+        carry = group(0, (carry, None), True)
+        carry = lax.fori_loop(1, NCH // PAIR, lambda i, x: group(i, x, False), carry)
+        if e != HID2:
+            send_ends(e)
+        return carry[0]
+
+    centers_of = {HID1: mcs1, HID2: mcs, SLO1: mcs}
+
+    def keep_chunk(e, c, vs, center, tile, inner):
+        vs = [v - center for v in vs]
+        pack(e, c, vs, tile)
+        if e != SLO1:
+            hc = hc1 if e == HID1 else hc2
+            for k, v in enumerate(vs):
+                hc[pl.ds(row_of(c * CH + k), R), :] = v
+                inner = inner + eight(v * v)
+        return inner
+
+    def forward_loop(vo, vh, w_ref, e, before):
+        def step(c, slot, squares):
+            return squares, conv_rows(vo, vh, w_ref, c, slot)
+
+        squares = fold(one(paired(e, step, zero8, before)))
+        centers = centers_of[e][...]
         mean = one(scs[...]) / cells
-        off = centers[...] - mean
-        rest = scs[...] - (4.0 * CR) * centers[...]
+        off = centers - mean
+        rest = scs[...] - (4.0 * CR) * centers
         spread = squares + one(off * (2.0 * rest + (4.0 * CR) * off))
         return mean, spread
 
@@ -548,13 +630,19 @@
         variance = (sums[1:2] + cells * between) / total
         return center, lax.rsqrt(variance + EPSILON)
 
+    fetch[0].wait()
     build(k1_ref, wf1, True)
+    fetch[1].wait()
     enter(f_ref, vo_f, FEAT)
     pl.semaphore_wait(barrier, n - 1)
     send_all(FEAT)
+    fetch[2].wait()
     build(k2_ref, wf2, True)
+    build(k2_ref, wb2, False)
+    build(k1_ref, wb1, False)
+    fetch[3].wait()
     enter(c_ref, vo_c, COT)
-    flip(vo_f, vt_f)
+    forward(FEAT, ODD)
 
     def put_f(dst):
         def use(row, value, center, keep):
@@ -566,22 +654,37 @@
     each_end(FEAT, put_f(vh_f), put_f(vo_f))
 
     def take_f(c):
-        arrive(side_copies(FEAT, c))
         found, _ = halo_rows(FEAT, c)
         for k, value in enumerate(found):
             put_f(vh_f)(row_of(c * CH + k + 1), value, None, keep_h)
 
+    arrive(side_copies(FEAT, 0))
     take_f(0)
 
-    def before_f(c):
-        @pl.when(c < NCH - 1)
+    def before_f(i):
+        low = i * PAIR + 1
+        high = jnp.minimum(low + 1, NCH - 1)
+        arrive(side_copies(FEAT, low))
+
+        @pl.when(high > low)
         def _():
-            take_f(c + 1)
-
-    mean, spread = forward_loop(vo_f, vh_f, wf1, hc1, mcs1, HID1, before_f)
+            arrive(side_copies(FEAT, high))
+
+        take_f(low)
+        take_f(high)
+
+    mean, spread = forward_loop(vo_f, vh_f, wf1, HID1, before_f)
     stats_send(0, mean, spread)
-    build(k2_ref, wb2, False)
-    build(k1_ref, wb1, False)
+    for copy in fetch[4:]:
+        copy.wait()
+    par[...] = jnp.zeros(par.shape, F32)
+    for row, ref in enumerate((g1_ref, b1_ref, g2_ref, b2_ref)):
+        par[row : row + 1, 0:C] = ref[...]
+    params = fold(par[...])
+    gain1, bias1, gain2, bias2 = [params[r : r + 1] for r in range(4)]
+    forward(HID1, ODD[: NCH // 4])
+    flip(vo_f, vt_f)
+    forward(HID1, ODD[NCH // 4 :])
     center, inv1 = moments(0)
     arrive_all(HID1)
     send_all(COT)
@@ -605,10 +708,13 @@
 
     lax.fori_loop(0, NCH, own_active, 0)
     each_halo(HID1, put_a(n1h, vh_a, inv1, gain1, bias1, center), own_a)
-
-    mean, spread = forward_loop(vo_a, vh_a, wf2, hc2, mcs, HID2, lambda c: None)
+    forward(COT, ODD)
+
+    mean, spread = forward_loop(vo_a, vh_a, wf2, HID2, None)
     stats_send(1, mean, spread)
+    send_all(HID2)
     flip(vo_a, vt_a)
+    forward(HID2, ODD)
     center, inv2 = moments(1)
 
     def own_output(c, carry):
@@ -675,10 +781,10 @@
     for side in range(2):
         grad_rows(END[side] * R, keep_o[side], keep_ho[side])
 
-    def back_loop(c, carry):
+    def back_step(c, slot, carry):
         plain, along = carry
         slopes = []
-        for k, back in enumerate(conv_rows(vo_g, vh_g, wb2, c)):
+        for k, back in enumerate(conv_rows(vo_g, vh_g, wb2, c, slot)):
             rows = pl.ds(row_of(c * CH + k + 1), R)
             normed = n1o[rows, :]
             slope = back * activate_slope(normed * gain1 + bias1)
@@ -686,16 +792,16 @@
             plain = plain + eight(slope)
             along = along + eight(slope * normed)
             slopes.append(slope)
-        _, mid, tile = centered(slopes)
-        pack(SLO1, c, [v - mid for v in slopes], tile)
-        send(SLO1, c)
-        return plain, along
-
-    plain, along = lax.fori_loop(0, NCH, back_loop, (zero8, zero8))
+        return (plain, along), slopes
+
+    plain, along = paired(SLO1, back_step, (zero8, zero8))
     stats_send(3, fold(one(plain)), fold(one(along)))
+    forward(SLO1, ODD[: NCH // 4])
     kernel_terms(1, vt_a, vo_g, vh_g)
+    forward(SLO1, ODD[NCH // 4 :])
     sums1 = stats_wait(3)
     arrive_all(SLO1)
+    pieces_sum(1)
     factor1 = gain1 * inv1
 
     def put_g(dst, normed_ref):
@@ -715,23 +821,42 @@
     lax.fori_loop(0, NCH, grad_one, 0)
     each_halo(SLO1, put_g(vh_g, n1h), put_g(vo_g, n1o))
     kernel_terms(0, vt_f, vo_g, vh_g)
-    pieces_sum(1)
-
-    def last_loop(c, carry):
-        for k, back in enumerate(conv_rows(vo_g, vh_g, wb1, c)):
-            outb[pl.ds(row_of(c * CH + k), R), :] = back.astype(BF16)
+
+    def last_loop(i, carry):
+        for j in range(PAIR):
+            c = i * PAIR + j
+            for k, back in enumerate(conv_rows(vo_g, vh_g, wb1, c, j * CH)):
+                outb[pl.ds(row_of(c * CH + k), R), :] = back.astype(BF16)
         return carry
 
-    lax.fori_loop(0, NCH, last_loop, 0)
+    lax.fori_loop(0, NCH // PAIR, last_loop, 0)
     pieces_sum(0)
     leave(outb, fg_ref)
-    scale = 1.0 / (total ** 0.5)
     for row, (sums, part) in enumerate(((sums1, 1), (sums1, 0), (sums2, 1), (sums2, 0))):
-        ng_ref[row : row + 1, :] = sums[part : part + 1, 0:C] * scale
-    pieces_out(1, dk2_ref, scale)
-    pieces_out(0, dk1_ref, scale)
+        ng_ref[row : row + 1, :] = sums[part : part + 1]
+    pieces_out(1)
+    pieces_out(0)
     for e in range(NEXCH):
         sent_all(e)
+        forwarded(e)
+
+
+def finish(scale, o_ref, fg_ref, dk_ref, ng_ref, oo_ref, ofg_ref, dk1_ref, dk2_ref, ong_ref, sem):
+    C = o_ref.shape[0]
+    copies = [
+        pltpu.make_async_copy(o_ref, oo_ref, sem.at[0]),
+        pltpu.make_async_copy(fg_ref, ofg_ref, sem.at[1]),
+    ]
+    for copy in copies:
+        copy.start()
+    for w, out_ref in enumerate((dk1_ref, dk2_ref)):
+        for group in range(7):
+            tall = jnp.transpose(dk_ref[w, group * C : (group + 1) * C].astype(F32)) * scale
+            for slot in range(min(4, 27 - 4 * group)):
+                out_ref[4 * group + slot] = tall[slot * C : (slot + 1) * C]
+    ong_ref[...] = ng_ref[0:4, 0:C] * scale
+    for copy in copies:
+        copy.wait()
 
 
 def local(features, kernel_one, gain_one, bias_one, kernel_two, gain_two, bias_two, cotangent):
@@ -758,36 +883,55 @@
     scratch += [V((rows, L), F32)] * 2
     scratch += [V((all_rows, L), F32)] * 7
     scratch += [
-        V((rows, L), BF16), V((CH, R + 16, L), F32), V((NCH, L), F32), V((NCH, L), F32),
+        V((rows, L), BF16), V((2 * CH, R + 16, L), F32), V((NCH, L), F32), V((NCH, L), F32),
         V((NCH, L), F32), V((3, 2 * L, 2 * L), F32),
     ]
-    scratch += [V((NEXCH, NCH, packed, L), BF16)] * 2 + [V((NEXCH, 2, R + 16, L), BF16)]
+    scratch += [V((NEXCH, NCH, packed, L), BF16)] * 2 + [V((NEXCH, 3, R + 16, L), BF16)]
     scratch += [V((NEXCH, NCH, packed, L), BF16)] * 2 + [V((NEXCH, 2, R + 16, L), BF16)] * 3
     scratch += [DMA((NEXCH, 2 * NCH + 6))] * 2
-    scratch += [V((4, 2, L), F32), V((4, n, 2, L), F32), DMA((2, n)), DMA((2, n))]
+    scratch += [V((4, 2, L), F32), V((4, n, 2, L), F32), DMA((4,)), DMA((4,))]
     scratch += [
-        V((2, n, piece, L), F32), V((2, n, piece, L), F32), V((2, piece, L), F32),
-        V((2, n, piece, L), F32), DMA((2, 2, n)), DMA((2, 2, n)),
+        V((2, n, piece, L), F32), V((2, n, piece, L), F32), V((2, piece, L), BF16),
+        V((2, n, piece, L), BF16), DMA((2, 2)), DMA((2, 2)),
+        V((C, X, Y, Z), BF16), V((C, X, Y, Z), BF16), V((27, C, C), BF16), V((27, C, C), BF16),
+        *[V((1, C), F32)] * 4, DMA((8,)), V((NEXCH, NCH // 2, packed, L), BF16),
+        DMA((NEXCH, NCH // 2)), DMA((NEXCH, NCH // 2)),
     ]
     vmem = pl.BlockSpec(memory_space=pltpu.VMEM)
-    out, fg, dk1, dk2, norm = pl.pallas_call(
+    anywhere = pl.BlockSpec(memory_space=pl.ANY)
+    volume = jax.ShapeDtypeStruct((C, X, Y, Z), BF16)
+    mids = pl.pallas_call(
         functools.partial(kernel, nx, ny, total),
         name="blocks",
         out_shape=[
-            jax.ShapeDtypeStruct((C, X, Y, Z), BF16), jax.ShapeDtypeStruct((C, X, Y, Z), BF16),
-            jax.ShapeDtypeStruct((27, C, C), F32), jax.ShapeDtypeStruct((27, C, C), F32),
-            jax.ShapeDtypeStruct((4, C), F32),
+            volume, volume, jax.ShapeDtypeStruct((2, n * piece, L), BF16),
+            jax.ShapeDtypeStruct((8, L), F32),
         ],
-        in_specs=[vmem] * 8,
-        out_specs=[vmem] * 5,
+        in_specs=[pl.BlockSpec(memory_space=pltpu.HBM)] * 8,
+        out_specs=[vmem] * 4,
         scratch_shapes=scratch,
         compiler_params=pltpu.CompilerParams(
-            collective_id=0, has_side_effects=True, vmem_limit_bytes=62 << 20
+            collective_id=0, has_side_effects=True, vmem_limit_bytes=48 << 20
         ),
     )(
-        features, cotangent, taps(kernel_one), taps(kernel_two),
-        row(gain_one), row(bias_one), row(gain_two), row(bias_two),
+        *[
+            pltpu.with_memory_space_constraint(v, pltpu.HBM)
+            for v in (
+                features, cotangent, taps(kernel_one), taps(kernel_two),
+                row(gain_one), row(bias_one), row(gain_two), row(bias_two),
+            )
+        ]
     )
+    terms = jax.ShapeDtypeStruct((27, C, C), F32)
+    out, fg, dk1, dk2, norm = pl.pallas_call(
+        functools.partial(finish, total ** -0.5),
+        name="finish",
+        out_shape=[volume, volume, terms, terms, jax.ShapeDtypeStruct((4, C), F32)],
+        in_specs=[anywhere] * 2 + [vmem] * 2,
+        out_specs=[anywhere] * 2 + [vmem] * 3,
+        scratch_shapes=[DMA((2,))],
+        compiler_params=pltpu.CompilerParams(vmem_limit_bytes=8 << 20),
+    )(*mids)
     untap = lambda d: jnp.transpose(d.reshape(3, 3, 3, C, C), (3, 4, 0, 1, 2))
     return out, fg, untap(dk1), untap(dk2), norm
 

time: 96.3 us -> 67.8 us (0.70)
  Pallas kernels: 89.7 us -> 67 us
  local copies, waits for them, and re-layouts: 5.65 us -> 0 us
    pallas_call x1, Pallas kernels: 89.7 us -> 65.1 us  [local(): pl.pallas_call(functools.partial(kernel, nx, ny, total), name='blocks', o...]
    unnamed x13 -> x0, local copies, waits for them, and re-layouts: 5.65 us -> none
    pallas_call x0 -> x1, Pallas kernels: none -> 1.9 us  [local(): pl.pallas_call(functools.partial(finish, total ** (-0.5)), name='finish',...]
where the time goes in v2:
time: 67.8 us; the launch traced here: 67.6 us
  Pallas kernels  67 us (99%)
    pallas_call x1, Pallas kernels, local(): pl.pallas_call(functools.partial(kernel, nx, ny, total), name='blocks', o...  65.1 us
    pallas_call x1, Pallas kernels, local(): pl.pallas_call(functools.partial(finish, total ** (-0.5)), name='finish',...  1.9 us

profile of v2, /device:TPU:0, one launch (start us, length us, event | category | flops | bytes accessed | tf_op | source)
XLA Modules:
  0.0 67.6 jit_solution(9863438664913219550)
XLA Ops:
  0.6 65.1 %blocks.1 = (bf16[32,2,32,128]{3,2,1,0:T(8,128)(2,1)S(1)}, bf16[32,2,32,128]{3,2,1,0:T(8,128)(2,1)S(1)}, bf16[2,256,128]{2,1,0:T(8,128)(2,1)S(1)}, f32[8,128]{1,0:T(8,128)S(1)}) custom-call(bf16[32,2,32,128]{3,2,1,0:T(8,128)(2,1)} %f_hbm.1, bf16[32,2,32,128]{3,2,1,0:T(8,128)(2,1)} %c_hbm.1, bf16[27,32,32]{2,1,0:T(8,128)(2,1)} %bitcast.16, ...), custom_call_target="tpu_custom_call" | custom-call | tf_op jit(solution)/shard_map/blocks/pallas_call | solution.py:903
  65.7 1.9 %finish.1 = (bf16[32,2,32,128]{3,2,1,0:T(8,128)(2,1)}, bf16[32,2,32,128]{3,2,1,0:T(8,128)(2,1)}, f32[27,32,32]{2,1,0:T(8,128)}, f32[27,32,32]{2,1,0:T(8,128)}, f32[4,32]{1,0:T(4,128)}) custom-call(bf16[32,2,32,128]{3,2,1,0:T(8,128)(2,1)S(1)} %get-tuple-element.14.o_ref, bf16[32,2,32,128]{3,2,1,0:T(8,128)(2,1)S(1)} %get-tuple-element.15.fg_ref, ...), custom_call_target="tpu_custom_call" | custom-call | tf_op jit(solution)/shard_map/finish/pallas_call | solution.py:926

commit v3 on v2

--- a/solution.py
+++ b/solution.py
@@ -32,10 +32,18 @@
     return (SLOPE + half) + half * jnp.tanh((0.5 * SHARPNESS) * s)
 
 
+def untap(flat, out_ref, scale):
+    C = out_ref.shape[1]
+    for group in range(7):
+        tall = jnp.transpose(flat[group * C : (group + 1) * C].astype(F32)) * scale
+        for slot in range(min(4, 27 - 4 * group)):
+            out_ref[4 * group + slot] = tall[slot * C : (slot + 1) * C]
+
+
 def kernel(
     nx, ny, total,
     f_hbm, c_hbm, k1_hbm, k2_hbm, g1_hbm, b1_hbm, g2_hbm, b2_hbm,
-    o_ref, fg_ref, dk_ref, ng_ref,
+    o_ref, fg_ref, dk1_ref, dk2_ref, ng_ref,
     t1, par, e_mat, s_mat, i_mat, base, wf1, wf2, wb2, wb1,
     vo_f, vh_f, vo_c, vh_c, vo_a, vh_a, vo_g, vh_g, vt_f, vt_a,
     hc1, hc2, n1o, n1h, n2o, n2h, s2o, s2h, s1o, outb, bs, mcs, scs, mcs1, raw,
@@ -59,11 +67,22 @@
         other = me + k
         return jnp.where(other >= n, other - n, other)
 
+    def others(use):
+        if n & (n - 1):
+            lax.fori_loop(1, n, lambda k, carry: (use(peer(k)), carry)[1], 0)
+            return
+        for dy in range(ny - 1, -1, -1):
+            def body(t, carry, dy=dy):
+                use(jnp.bitwise_xor(me, (nx - 1 - t) * ny + dy))
+                return carry
+
+            lax.fori_loop(0, nx if dy else nx - 1, body, 0)
+
     fetch = [
         pltpu.make_async_copy(src, dst, in_sem.at[k])
         for k, (src, dst) in enumerate(
             (
-                (k1_hbm, k1_ref), (f_hbm, f_ref), (k2_hbm, k2_ref), (c_hbm, c_ref),
+                (f_hbm, f_ref), (k1_hbm, k1_ref), (k2_hbm, k2_ref), (c_hbm, c_ref),
                 (g1_hbm, g1_ref), (b1_hbm, b1_ref), (g2_hbm, g2_ref), (b2_hbm, b2_ref),
             )
         )
@@ -73,11 +92,9 @@
 
     barrier = pltpu.get_barrier_semaphore()
 
-    def hello(k, carry):
-        pl.semaphore_signal(barrier, inc=1, device_id=peer(k), device_id_type=LOGICAL)
-        return carry
-
-    lax.fori_loop(1, n, hello, 0)
+    others(
+        lambda d: pl.semaphore_signal(barrier, inc=1, device_id=d, device_id_type=LOGICAL)
+    )
 
     lane = lax.broadcasted_iota(jnp.int32, (1, L), 1)
     xb = lax.rem(lane // C, 2) == 1
@@ -166,7 +183,7 @@
 
         lax.fori_loop(0, 3, one_row, 0)
 
-    def enter(in_ref, vo, e):
+    def enter(in_ref, vo, e, after=None):
         def widen(c, carry):
             t1[pl.ds(pl.multiple_of(c * X * Y, X * Y), X * Y), :] = (
                 in_ref[c].reshape(X * Y, Z).astype(F32)
@@ -193,7 +210,13 @@
             pack(e, c, vs, None)
             return carry
 
-        loop(NCH, chunk, unroll=2)
+        for part in range(2):
+            lax.fori_loop(
+                part * NCH // 4, (part + 1) * NCH // 4,
+                lambda h, carry: chunk(2 * h + 1, chunk(2 * h, carry)), 0,
+            )
+            if after is not None:
+                after(part)
 
     def leave(src, dst):
         def pair(p, carry):
@@ -250,7 +273,7 @@
             spr[e, c, R : R + 16, :] = center
             spl[e, c, R : R + 16, :] = center
 
-        first = jnp.where(c == 0, 0, 2)
+        first = 2 if isinstance(c, int) and c else jnp.where(c == 0, 0, 2)
         se[e, first, 0:R, :] = vs[0].astype(BF16)
         if center is not None:
             se[e, first, R : R + 16, :] = center
@@ -368,13 +391,16 @@
         for copies in end_copies(e):
             start(copies)
 
-    def send_all(e):
+    def send_part(e, low, high):
         def body(h, carry):
             send(e, 2 * h, False)
             send(e, 2 * h + 1, True)
             return carry
 
-        lax.fori_loop(0, NCH // 2, body, 0)
+        lax.fori_loop(low, high, body, 0)
+
+    def send_all(e):
+        send_part(e, 0, NCH // 2)
         send_ends(e)
 
     def arrive_ends(e):
@@ -451,49 +477,46 @@
         msg[r] = both
         st[r, me] = both
 
-        def body(k, carry):
-            pltpu.make_async_remote_copy(
+        others(
+            lambda d: pltpu.make_async_remote_copy(
                 src_ref=msg.at[r], dst_ref=st.at[r, me],
                 send_sem=ss_sem.at[r], recv_sem=sr_sem.at[r],
-                device_id=peer(k), device_id_type=LOGICAL,
+                device_id=d, device_id_type=LOGICAL,
             ).start()
-            return carry
-
-        lax.fori_loop(1, n, body, 0)
+        )
 
     def stats_wait(r):
-        others = st.at[r, pl.ds(0, n - 1)]
+        rest = st.at[r, pl.ds(0, n - 1)]
         pltpu.make_async_remote_copy(
-            src_ref=others, dst_ref=others, send_sem=ss_sem.at[r], recv_sem=sr_sem.at[r],
+            src_ref=rest, dst_ref=rest, send_sem=ss_sem.at[r], recv_sem=sr_sem.at[r],
             device_id=peer(1), device_id_type=LOGICAL,
         ).wait()
         return jnp.sum(st[r], axis=0)
 
     def pieces_send(w, phase):
-        def body(k, carry):
-            other = peer(k)
-            pltpu.make_async_remote_copy(
-                src_ref=pk.at[w, other] if phase == 0 else ags.at[w],
+        others(
+            lambda d: pltpu.make_async_remote_copy(
+                src_ref=pk.at[w, d] if phase == 0 else ags.at[w],
                 dst_ref=(rsb if phase == 0 else agb).at[w, me],
                 send_sem=ws_sem.at[w, phase], recv_sem=wr_sem.at[w, phase],
-                device_id=other, device_id_type=LOGICAL,
+                device_id=d, device_id_type=LOGICAL,
             ).start()
-            return carry
-
-        lax.fori_loop(1, n, body, 0)
+        )
 
     def pieces_wait(w, phase):
-        others = (rsb if phase == 0 else agb).at[w, pl.ds(0, n - 1)]
+        rest = (rsb if phase == 0 else agb).at[w, pl.ds(0, n - 1)]
         pltpu.make_async_remote_copy(
-            src_ref=others, dst_ref=others,
+            src_ref=rest, dst_ref=rest,
             send_sem=ws_sem.at[w, phase], recv_sem=wr_sem.at[w, phase],
             device_id=peer(1), device_id_type=LOGICAL,
         ).wait()
 
-    def kernel_terms(w, vt, vo, vh):
+    def kernel_products(vt, vo, vh):
         for j in range(3):
             g = jnp.concatenate([vo[j * R : (j + Y) * R, :], vh[j * R : (j + Y) * R, :]], axis=1)
             raw[j] = jnp.dot(vt[...], g, preferred_element_type=F32)
+
+    def kernel_terms(w):
         block = lax.broadcasted_iota(jnp.int32, (C, L), 1) // C
         rows_v = cols_a + cols_b
         groups = [jnp.zeros((C, L), F32) for _ in range(7)]
@@ -522,7 +545,6 @@
             flat = jnp.concatenate([flat, jnp.zeros((rows - flat.shape[0], L), F32)], axis=0)
         pk[w] = flat.reshape(n, PIECE, L)
         rsb[w, me] = pk[w, me]
-        pieces_send(w, 0)
 
     def pieces_sum(w):
         pieces_wait(w, 0)
@@ -531,9 +553,11 @@
         agb[w, me] = whole
         pieces_send(w, 1)
 
+    dk_refs = (dk1_ref, dk2_ref)
+
     def pieces_out(w):
         pieces_wait(w, 1)
-        dk_ref[w] = agb[w].reshape(n * PIECE, L)
+        untap(agb[w].reshape(n * PIECE, L), dk_refs[w], total ** -0.5)
 
     def conv_rows(vo, vh, w_ref, c, slot=0):
         parts = []
@@ -568,7 +592,7 @@
     zero8 = jnp.zeros((8, L), F32)
     PAIR = 2
 
-    def paired(e, step, carry, before=None):
+    def paired(e, step, carry, before=None, after=None):
         def group(i, carry, first):
             inner, s = carry
             if before is not None:
@@ -577,22 +601,31 @@
             for k in range(PAIR):
                 inner, vs = step(i * PAIR + k, k * CH, inner)
                 found.append((vs, totals(vs)))
+            if after is not None:
+                after(i)
             center, tile = center_near(found[0][1] if first else s)
             for k, (vs, s) in enumerate(found):
                 c = i * PAIR + k
                 centers_of[e][pl.ds(c, 1), :] = center
                 scs[pl.ds(c, 1), :] = s
                 inner = keep_chunk(e, c, vs, center, tile, inner)
-            if e != HID2:
+            if e != HID2 and i < EARLY:
                 for k in range(PAIR):
                     send(e, i * PAIR + k, k % 2 == 1)
             return inner, s
 
         carry = group(0, (carry, None), True)
-        carry = lax.fori_loop(1, NCH // PAIR, lambda i, x: group(i, x, False), carry)
-        if e != HID2:
-            send_ends(e)
+        for i in range(1, NCH // PAIR):
+            carry = group(i, carry, False)
         return carry[0]
+
+    EARLY = NCH // PAIR // 2
+
+    def send_late(e):
+        for i in range(EARLY, NCH // PAIR):
+            for k in range(PAIR):
+                send(e, i * PAIR + k, k % 2 == 1)
+        send_ends(e)
 
     centers_of = {HID1: mcs1, HID2: mcs, SLO1: mcs}
 
@@ -606,11 +639,11 @@
                 inner = inner + eight(v * v)
         return inner
 
-    def forward_loop(vo, vh, w_ref, e, before):
+    def forward_loop(vo, vh, w_ref, e, before=None, after=None):
         def step(c, slot, squares):
             return squares, conv_rows(vo, vh, w_ref, c, slot)
 
-        squares = fold(one(paired(e, step, zero8, before)))
+        squares = fold(one(paired(e, step, zero8, before, after)))
         centers = centers_of[e][...]
         mean = one(scs[...]) / cells
         off = centers - mean
@@ -631,18 +664,24 @@
         return center, lax.rsqrt(variance + EPSILON)
 
     fetch[0].wait()
+
+    def send_f(part):
+        if part == 0:
+            pl.semaphore_wait(barrier, n - 1)
+        send_part(FEAT, part * NCH // 4, (part + 1) * NCH // 4)
+
+    enter(f_ref, vo_f, FEAT, send_f)
+    send_ends(FEAT)
+    fetch[1].wait()
     build(k1_ref, wf1, True)
-    fetch[1].wait()
-    enter(f_ref, vo_f, FEAT)
-    pl.semaphore_wait(barrier, n - 1)
-    send_all(FEAT)
     fetch[2].wait()
     build(k2_ref, wf2, True)
     build(k2_ref, wb2, False)
     build(k1_ref, wb1, False)
     fetch[3].wait()
+    forward(FEAT, ODD[: NCH // 4])
     enter(c_ref, vo_c, COT)
-    forward(FEAT, ODD)
+    forward(FEAT, ODD[NCH // 4 :])
 
     def put_f(dst):
         def use(row, value, center, keep):
@@ -662,19 +701,13 @@
     take_f(0)
 
     def before_f(i):
-        low = i * PAIR + 1
-        high = jnp.minimum(low + 1, NCH - 1)
-        arrive(side_copies(FEAT, low))
-
-        @pl.when(high > low)
-        def _():
-            arrive(side_copies(FEAT, high))
-
-        take_f(low)
-        take_f(high)
+        for c in range(i * PAIR + 1, min(i * PAIR + PAIR + 1, NCH)):
+            arrive(side_copies(FEAT, c))
+            take_f(c)
 
     mean, spread = forward_loop(vo_f, vh_f, wf1, HID1, before_f)
     stats_send(0, mean, spread)
+    send_late(HID1)
     for copy in fetch[4:]:
         copy.wait()
     par[...] = jnp.zeros(par.shape, F32)
@@ -682,12 +715,11 @@
         par[row : row + 1, 0:C] = ref[...]
     params = fold(par[...])
     gain1, bias1, gain2, bias2 = [params[r : r + 1] for r in range(4)]
-    forward(HID1, ODD[: NCH // 4])
     flip(vo_f, vt_f)
-    forward(HID1, ODD[NCH // 4 :])
+    forward(HID1, ODD)
+    send_all(COT)
     center, inv1 = moments(0)
     arrive_all(HID1)
-    send_all(COT)
 
     def put_a(n_dst, v_dst, inv, gain, bias, center):
         def use(row, value, mid, keep):
@@ -700,21 +732,29 @@
 
     own_a = put_a(n1o, vo_a, inv1, gain1, bias1, center)
 
-    def own_active(c, carry):
-        mid = mcs1[pl.ds(c, 1), :]
+    halo_a = put_a(n1h, vh_a, inv1, gain1, bias1, center)
+
+    def active_chunk(c):
+        mid = mcs1[c : c + 1, :]
         for k in range(CH):
             own_a(row_of(c * CH + k + 1), hc1[pl.ds(row_of(c * CH + k), R), :], mid, None)
-        return carry
-
-    lax.fori_loop(0, NCH, own_active, 0)
-    each_halo(HID1, put_a(n1h, vh_a, inv1, gain1, bias1, center), own_a)
-    forward(COT, ODD)
-
-    mean, spread = forward_loop(vo_a, vh_a, wf2, HID2, None)
+        found, mid = halo_rows(HID1, c)
+        for k, value in enumerate(found):
+            halo_a(row_of(c * CH + k + 1), value, mid, keep_h)
+
+    def after_a(i):
+        for c in range(PAIR * (i + 1) + 1, min(PAIR * (i + 2) + 1, NCH)):
+            active_chunk(c)
+
+    each_end(HID1, halo_a, own_a)
+    for c in range(min(PAIR + 1, NCH)):
+        active_chunk(c)
+
+    mean, spread = forward_loop(vo_a, vh_a, wf2, HID2, after=after_a)
     stats_send(1, mean, spread)
     send_all(HID2)
     flip(vo_a, vt_a)
-    forward(HID2, ODD)
+    forward(COT, ODD)
     center, inv2 = moments(1)
 
     def own_output(c, carry):
@@ -736,6 +776,8 @@
     plain, along = lax.fori_loop(0, NCH, own_output, (zero8, zero8))
     stats_send(2, fold(one(plain)), fold(one(along)))
 
+    forward(HID2, ODD)
+    leave(outb, o_ref)
     arrive_all(COT)
     arrive_all(HID2)
 
@@ -757,7 +799,6 @@
         return use
 
     each_halo(HID2, put_s(n2h, s2h, vh_c), put_s(n2o, s2o, vo_c))
-    leave(outb, o_ref)
     sums2 = stats_wait(2)
 
     def gradient(slope, normed, sums, factor):
@@ -796,12 +837,14 @@
 
     plain, along = paired(SLO1, back_step, (zero8, zero8))
     stats_send(3, fold(one(plain)), fold(one(along)))
+    send_late(SLO1)
+    kernel_products(vt_a, vo_g, vh_g)
     forward(SLO1, ODD[: NCH // 4])
-    kernel_terms(1, vt_a, vo_g, vh_g)
+    kernel_terms(1)
     forward(SLO1, ODD[NCH // 4 :])
     sums1 = stats_wait(3)
     arrive_all(SLO1)
-    pieces_sum(1)
+    pieces_send(1, 0)
     factor1 = gain1 * inv1
 
     def put_g(dst, normed_ref):
@@ -820,7 +863,9 @@
 
     lax.fori_loop(0, NCH, grad_one, 0)
     each_halo(SLO1, put_g(vh_g, n1h), put_g(vo_g, n1o))
-    kernel_terms(0, vt_f, vo_g, vh_g)
+    kernel_products(vt_f, vo_g, vh_g)
+    kernel_terms(0)
+    pieces_send(0, 0)
 
     def last_loop(i, carry):
         for j in range(PAIR):
@@ -829,32 +874,28 @@
                 outb[pl.ds(row_of(c * CH + k), R), :] = back.astype(BF16)
         return carry
 
-    lax.fori_loop(0, NCH // PAIR, last_loop, 0)
+    for i in range(NCH // PAIR):
+        last_loop(i, 0)
+    pieces_sum(1)
     pieces_sum(0)
     leave(outb, fg_ref)
     for row, (sums, part) in enumerate(((sums1, 1), (sums1, 0), (sums2, 1), (sums2, 0))):
-        ng_ref[row : row + 1, :] = sums[part : part + 1]
-    pieces_out(1)
-    pieces_out(0)
+        ng_ref[row : row + 1, :] = sums[part : part + 1, 0:C] * total ** -0.5
     for e in range(NEXCH):
         sent_all(e)
         forwarded(e)
-
-
-def finish(scale, o_ref, fg_ref, dk_ref, ng_ref, oo_ref, ofg_ref, dk1_ref, dk2_ref, ong_ref, sem):
-    C = o_ref.shape[0]
+    pieces_out(1)
+    pieces_out(0)
+
+
+def finish(o_ref, fg_ref, dk1_ref, dk2_ref, ng_ref, *rest):
+    outs, sem = rest[:-1], rest[-1]
     copies = [
-        pltpu.make_async_copy(o_ref, oo_ref, sem.at[0]),
-        pltpu.make_async_copy(fg_ref, ofg_ref, sem.at[1]),
+        pltpu.make_async_copy(src, dst, sem.at[k])
+        for k, (src, dst) in enumerate(zip((o_ref, fg_ref, dk1_ref, dk2_ref, ng_ref), outs))
     ]
     for copy in copies:
         copy.start()
-    for w, out_ref in enumerate((dk1_ref, dk2_ref)):
-        for group in range(7):
-            tall = jnp.transpose(dk_ref[w, group * C : (group + 1) * C].astype(F32)) * scale
-            for slot in range(min(4, 27 - 4 * group)):
-                out_ref[4 * group + slot] = tall[slot * C : (slot + 1) * C]
-    ong_ref[...] = ng_ref[0:4, 0:C] * scale
     for copy in copies:
         copy.wait()
 
@@ -899,16 +940,16 @@
     ]
     vmem = pl.BlockSpec(memory_space=pltpu.VMEM)
     anywhere = pl.BlockSpec(memory_space=pl.ANY)
+    terms = jax.ShapeDtypeStruct((27, C, C), F32)
     volume = jax.ShapeDtypeStruct((C, X, Y, Z), BF16)
     mids = pl.pallas_call(
         functools.partial(kernel, nx, ny, total),
         name="blocks",
         out_shape=[
-            volume, volume, jax.ShapeDtypeStruct((2, n * piece, L), BF16),
-            jax.ShapeDtypeStruct((8, L), F32),
+            volume, volume, terms, terms, jax.ShapeDtypeStruct((4, C), F32),
         ],
         in_specs=[pl.BlockSpec(memory_space=pltpu.HBM)] * 8,
-        out_specs=[vmem] * 4,
+        out_specs=[vmem] * 5,
         scratch_shapes=scratch,
         compiler_params=pltpu.CompilerParams(
             collective_id=0, has_side_effects=True, vmem_limit_bytes=48 << 20
@@ -922,18 +963,17 @@
             )
         ]
     )
-    terms = jax.ShapeDtypeStruct((27, C, C), F32)
     out, fg, dk1, dk2, norm = pl.pallas_call(
-        functools.partial(finish, total ** -0.5),
+        finish,
         name="finish",
         out_shape=[volume, volume, terms, terms, jax.ShapeDtypeStruct((4, C), F32)],
-        in_specs=[anywhere] * 2 + [vmem] * 2,
-        out_specs=[anywhere] * 2 + [vmem] * 3,
-        scratch_shapes=[DMA((2,))],
+        in_specs=[anywhere] * 5,
+        out_specs=[anywhere] * 5,
+        scratch_shapes=[DMA((5,))],
         compiler_params=pltpu.CompilerParams(vmem_limit_bytes=8 << 20),
     )(*mids)
-    untap = lambda d: jnp.transpose(d.reshape(3, 3, 3, C, C), (3, 4, 0, 1, 2))
-    return out, fg, untap(dk1), untap(dk2), norm
+    spatial = lambda d: jnp.transpose(d.reshape(3, 3, 3, C, C), (3, 4, 0, 1, 2))
+    return out, fg, spatial(dk1), spatial(dk2), norm
 
 
 def solution(mesh):

time: 67.8 us -> 60.9 us (0.90)
  Pallas kernels: 67 us -> 60.1 us
    pallas_call x1, Pallas kernels: 65.1 us -> 58.8 us  [local(): pl.pallas_call(functools.partial(kernel, nx, ny, total), name='blocks', o...]
where the time goes in v3:
time: 60.9 us; the launch traced here: 60.8 us
  Pallas kernels  60.1 us (99%)
  between operations  0.64 us (1%)
    pallas_call x1, Pallas kernels, local(): pl.pallas_call(functools.partial(kernel, nx, ny, total), name='blocks', o...  58.8 us
    pallas_call x1, Pallas kernels, local(): pl.pallas_call(finish, name='finish', out_shape=[volume, volume, terms, t...  1.3 us

profile of v3, /device:TPU:0, one launch (start us, length us, event | category | flops | bytes accessed | tf_op | source)
XLA Modules:
  0.0 60.8 jit_solution(15628235828219984571)
XLA Ops:
  0.6 58.8 %blocks.1 = (bf16[32,2,32,128]{3,2,1,0:T(8,128)(2,1)S(1)}, bf16[32,2,32,128]{3,2,1,0:T(8,128)(2,1)S(1)}, f32[27,32,32]{2,1,0:T(8,128)S(1)}, f32[27,32,32]{2,1,0:T(8,128)S(1)}, f32[4,32]{1,0:T(4,128)S(1)}) custom-call(bf16[32,2,32,128]{3,2,1,0:T(8,128)(2,1)} %f_hbm.1, bf16[32,2,32,128]{3,2,1,0:T(8,128)(2,1)} %c_hbm.1, bf16[27,32,32]{2,1,0:T(8,128)(2,1)} %bitcast.16, ...), custom_call_target="tpu_custom_call" | custom-call | tf_op jit(solution)/shard_map/blocks/pallas_call | solution.py:945
  59.5 1.3 %finish.1 = (bf16[32,2,32,128]{3,2,1,0:T(8,128)(2,1)}, bf16[32,2,32,128]{3,2,1,0:T(8,128)(2,1)}, f32[27,32,32]{2,1,0:T(8,128)}, f32[27,32,32]{2,1,0:T(8,128)}, f32[4,32]{1,0:T(4,128)}) custom-call(bf16[32,2,32,128]{3,2,1,0:T(8,128)(2,1)S(1)} %get-tuple-element.15.o_ref, bf16[32,2,32,128]{3,2,1,0:T(8,128)(2,1)S(1)} %get-tuple-element.16.fg_ref, ...), custom_call_target="tpu_custom_call" | custom-call | tf_op jit(solution)/shard_map/finish/pallas_call | solution.py:966

commit v4 on v3

--- a/solution.py
+++ b/solution.py
@@ -262,10 +262,17 @@
 
     half = CR // 2
 
+    def pair_rows(e, p):
+        low = p * (R + centre_rows(e))
+        return slice(low, low + R)
+
+    def centre_rows(e):
+        return 0 if e in (FEAT, COT) else 16
+
     def pack(e, c, vs, center):
         for p in range(CH // 2):
             a, b = vs[2 * p], vs[2 * p + 1]
-            rows = slice(p * (R + 16), p * (R + 16) + R)
+            rows = pair_rows(e, p)
             spr[e, c, rows, :] = jnp.where(xb, a, pltpu.roll(b, L - C, 1)).astype(BF16)
             spl[e, c, rows, :] = jnp.where(xb, pltpu.roll(b, C, 1), a).astype(BF16)
         if center is not None:
@@ -290,31 +297,35 @@
             device_id_type=MESH,
         )
 
+    def used(e, ref, c):
+        return ref.at[e, c, pl.ds(0, half + centre_rows(e))]
+
     def side_copies(e, c):
         return [
-            (has_r, has_l, copy_of(e, c, spr.at[e, c], rl.at[e, c], 1, 0)),
-            (has_l, has_r, copy_of(e, NCH + c, spl.at[e, c], rr.at[e, c], -1, 0)),
+            (has_r, has_l, copy_of(e, c, used(e, spr, c), used(e, rl, c), 1, 0)),
+            (has_l, has_r, copy_of(e, NCH + c, used(e, spl, c), used(e, rr, c), -1, 0)),
         ]
 
     def end_copies(e):
-        low, high = pl.ds(0, R + 16), pl.ds(R, R + 16)
+        size = R + centre_rows(e)
+        end, low, high = pl.ds(0, size), pl.ds(0, size), pl.ds(R, size)
         both = jnp.logical_and
         m = 2 * NCH
         last = NCH - 1
         return [
             [
-                (has_d, has_u, copy_of(e, m, se.at[e, 0], re.at[e, 1], 0, -1)),
+                (has_d, has_u, copy_of(e, m, se.at[e, 0, end], re.at[e, 1, end], 0, -1)),
                 (both(has_r, has_d), both(has_l, has_u),
-                 copy_of(e, m + 2, spr.at[e, 0, low], rdl.at[e, 1], 1, -1)),
+                 copy_of(e, m + 2, spr.at[e, 0, low], rdl.at[e, 1, end], 1, -1)),
                 (both(has_l, has_d), both(has_r, has_u),
-                 copy_of(e, m + 4, spl.at[e, 0, low], rdr.at[e, 1], -1, -1)),
+                 copy_of(e, m + 4, spl.at[e, 0, low], rdr.at[e, 1, end], -1, -1)),
             ],
             [
-                (has_u, has_d, copy_of(e, m + 1, se.at[e, 1], re.at[e, 0], 0, 1)),
+                (has_u, has_d, copy_of(e, m + 1, se.at[e, 1, end], re.at[e, 0, end], 0, 1)),
                 (both(has_r, has_u), both(has_l, has_d),
-                 copy_of(e, m + 3, spr.at[e, last, high], rdl.at[e, 0], 1, 1)),
+                 copy_of(e, m + 3, spr.at[e, last, high], rdl.at[e, 0, end], 1, 1)),
                 (both(has_l, has_u), both(has_r, has_d),
-                 copy_of(e, m + 5, spl.at[e, last, high], rdr.at[e, 0], -1, 1)),
+                 copy_of(e, m + 5, spl.at[e, last, high], rdr.at[e, 0, end], -1, 1)),
             ],
         ]
 
@@ -331,7 +342,7 @@
                 copy().wait_recv()
 
     RELAY = nx == 8
-    ODD = range(NCH // 2)
+    HALF = range(NCH // 2)
     low_mid, high_mid = nx // 2 - 1, nx // 2
 
     def hop(e, h, src, dst, there, s_sem, r_sem):
@@ -340,8 +351,8 @@
             device_id=(there, gy), device_id_type=MESH,
         )
 
-    def send_odd(e, c):
-        h = c // 2
+    def send_early(e, c):
+        h = c
         (_, _, right), (_, _, left) = side_copies(e, c)
         relays = (
             (gx == low_mid, has_r, right, spr, nx - 1, hs_sem.at[e, c]),
@@ -350,21 +361,21 @@
         for via, sends, direct, src, there, s_sem in relays:
             @pl.when(via)
             def _(src=src, there=there, s_sem=s_sem):
-                hop(e, h, src.at[e, c], rel.at[e, h], there, s_sem, rel_sem.at[e, h]).start()
+                hop(e, h, used(e, src, c), used(e, rel, h), there, s_sem, rel_sem.at[e, h]).start()
 
             @pl.when(jnp.logical_and(sends, jnp.logical_not(via)))
             def _(direct=direct):
                 direct().start()
 
     def forwards(e, h):
-        c = 2 * h + 1
+        c = h
         return (
-            (gx == nx - 1, hop(e, h, rel.at[e, h], rl.at[e, c], high_mid, fwd_sem.at[e, h], hr_sem.at[e, c])),
-            (gx == 0, hop(e, h, rel.at[e, h], rr.at[e, c], low_mid, fwd_sem.at[e, h], hr_sem.at[e, NCH + c])),
+            (gx == nx - 1, hop(e, h, used(e, rel, h), used(e, rl, c), high_mid, fwd_sem.at[e, h], hr_sem.at[e, c])),
+            (gx == 0, hop(e, h, used(e, rel, h), used(e, rr, c), low_mid, fwd_sem.at[e, h], hr_sem.at[e, NCH + c])),
         ) if RELAY else ()
 
     def relay_arrives(e, h):
-        hop(e, h, rel.at[e, h], rel.at[e, h], low_mid, fwd_sem.at[e, h], rel_sem.at[e, h]).wait_recv()
+        hop(e, h, used(e, rel, h), used(e, rel, h), low_mid, fwd_sem.at[e, h], rel_sem.at[e, h]).wait_recv()
 
     def forward(e, which):
         for h in which:
@@ -375,15 +386,15 @@
                     copy.start()
 
     def forwarded(e):
-        for h in ODD:
+        for h in HALF:
             for here, copy in forwards(e, h):
                 @pl.when(here)
                 def _(copy=copy):
                     copy.wait_send()
 
-    def send(e, c, odd):
-        if RELAY and odd:
-            send_odd(e, c)
+    def send(e, c, early):
+        if RELAY and early:
+            send_early(e, c)
         else:
             start(side_copies(e, c))
 
@@ -391,16 +402,16 @@
         for copies in end_copies(e):
             start(copies)
 
-    def send_part(e, low, high):
-        def body(h, carry):
-            send(e, 2 * h, False)
-            send(e, 2 * h + 1, True)
+    def send_part(e, part):
+        def body(c, carry):
+            send(e, c, part == 0)
             return carry
 
-        lax.fori_loop(low, high, body, 0)
+        lax.fori_loop(part * (NCH // 2), (part + 1) * (NCH // 2), body, 0)
 
     def send_all(e):
-        send_part(e, 0, NCH // 2)
+        send_part(e, 0)
+        send_part(e, 1)
         send_ends(e)
 
     def arrive_ends(e):
@@ -435,20 +446,28 @@
         return (wide[0:8] + wide[8:16])[0:1]
 
     def halo_rows(e, c):
-        center = jnp.where(xb, center_of(rl[e, c, R : R + 16, :]), center_of(rr[e, c, R : R + 16, :]))
+        center = None
+        if centre_rows(e):
+            tile = slice(R, R + 16)
+            center = jnp.where(xb, center_of(rl[e, c, tile, :]), center_of(rr[e, c, tile, :]))
         found = []
         for p in range(CH // 2):
-            rows = slice(p * (R + 16), p * (R + 16) + R)
+            rows = pair_rows(e, p)
             a, b = rl[e, c, rows, :].astype(F32), rr[e, c, rows, :].astype(F32)
             found.append(jnp.where(xb, a, b))
             found.append(jnp.where(xb, pltpu.roll(a, C, 1), pltpu.roll(b, L - C, 1)))
         return found, center
 
     def end_rows(e, side):
-        own, own_center = re[e, side, 0:R, :].astype(F32), center_of(re[e, side, R : R + 16, :])
-        data, tile = (slice(16, 16 + R), slice(0, 16)) if side == 0 else (slice(0, R), slice(R, R + 16))
+        own, own_center, center = re[e, side, 0:R, :].astype(F32), None, None
+        data = slice(0, R)
+        if centre_rows(e):
+            own_center = center_of(re[e, side, R : R + 16, :])
+            tile = slice(R, R + 16)
+            if side == 0:
+                data, tile = slice(16, 16 + R), slice(0, 16)
+            center = jnp.where(xb, center_of(rdl[e, side, tile, :]), center_of(rdr[e, side, tile, :]))
         a, b = rdl[e, side, data, :].astype(F32), rdr[e, side, data, :].astype(F32)
-        center = jnp.where(xb, center_of(rdl[e, side, tile, :]), center_of(rdr[e, side, tile, :]))
         if side == 0:
             a, b = pltpu.roll(a, C, 1), pltpu.roll(b, L - C, 1)
         return own, own_center, jnp.where(xb, a, b), center
@@ -462,7 +481,7 @@
                 use_halo(row_of(c * CH + k + 1), value, center, keep_h)
             return carry
 
-        lax.fori_loop(0, NCH, body, 0)
+        loop(NCH, body, unroll=2)
         each_end(e, use_halo, use_own)
 
     def each_end(e, use_halo, use_own):
@@ -609,9 +628,9 @@
                 centers_of[e][pl.ds(c, 1), :] = center
                 scs[pl.ds(c, 1), :] = s
                 inner = keep_chunk(e, c, vs, center, tile, inner)
-            if e != HID2 and i < EARLY:
+            if e != HID2 and i < early_groups(e):
                 for k in range(PAIR):
-                    send(e, i * PAIR + k, k % 2 == 1)
+                    send(e, i * PAIR + k, i < EARLY)
             return inner, s
 
         carry = group(0, (carry, None), True)
@@ -621,10 +640,13 @@
 
     EARLY = NCH // PAIR // 2
 
+    def early_groups(e):
+        return max(EARLY, NCH // PAIR - 1) if e == SLO1 else EARLY
+
     def send_late(e):
-        for i in range(EARLY, NCH // PAIR):
+        for i in range(early_groups(e), NCH // PAIR):
             for k in range(PAIR):
-                send(e, i * PAIR + k, k % 2 == 1)
+                send(e, i * PAIR + k, i < EARLY)
         send_ends(e)
 
     centers_of = {HID1: mcs1, HID2: mcs, SLO1: mcs}
@@ -655,11 +677,8 @@
         sums = stats_wait(r)
         center = sums[0:1] / n
 
-        def body(d, acc):
-            off = st[r, d] - center
-            return acc + off * off
-
-        between = lax.fori_loop(0, n, body, jnp.zeros((2, L), F32))[0:1]
+        off = st[r] - center
+        between = jnp.sum(off * off, axis=0)[0:1]
         variance = (sums[1:2] + cells * between) / total
         return center, lax.rsqrt(variance + EPSILON)
 
@@ -668,7 +687,7 @@
     def send_f(part):
         if part == 0:
             pl.semaphore_wait(barrier, n - 1)
-        send_part(FEAT, part * NCH // 4, (part + 1) * NCH // 4)
+        send_part(FEAT, part)
 
     enter(f_ref, vo_f, FEAT, send_f)
     send_ends(FEAT)
@@ -679,9 +698,8 @@
     build(k2_ref, wb2, False)
     build(k1_ref, wb1, False)
     fetch[3].wait()
-    forward(FEAT, ODD[: NCH // 4])
+    forward(FEAT, HALF)
     enter(c_ref, vo_c, COT)
-    forward(FEAT, ODD[NCH // 4 :])
 
     def put_f(dst):
         def use(row, value, center, keep):
@@ -716,9 +734,9 @@
     params = fold(par[...])
     gain1, bias1, gain2, bias2 = [params[r : r + 1] for r in range(4)]
     flip(vo_f, vt_f)
-    forward(HID1, ODD)
+    forward(HID1, HALF)
+    center, inv1 = moments(0)
     send_all(COT)
-    center, inv1 = moments(0)
     arrive_all(HID1)
 
     def put_a(n_dst, v_dst, inv, gain, bias, center):
@@ -752,9 +770,9 @@
 
     mean, spread = forward_loop(vo_a, vh_a, wf2, HID2, after=after_a)
     stats_send(1, mean, spread)
+    flip(vo_a, vt_a)
+    forward(COT, HALF)
     send_all(HID2)
-    flip(vo_a, vt_a)
-    forward(COT, ODD)
     center, inv2 = moments(1)
 
     def own_output(c, carry):
@@ -776,7 +794,7 @@
     plain, along = lax.fori_loop(0, NCH, own_output, (zero8, zero8))
     stats_send(2, fold(one(plain)), fold(one(along)))
 
-    forward(HID2, ODD)
+    forward(HID2, HALF)
     leave(outb, o_ref)
     arrive_all(COT)
     arrive_all(HID2)
@@ -813,12 +831,16 @@
         g = gradient(s2h[rows, :], n2h[rows, :], sums2, factor2)
         vh_g[rows, :] = jnp.where(keep_halo, g, 0.0).astype(BF16)
 
-    def grad_two(c, carry):
+    def grad_two(c):
         for k in range(CH):
             grad_rows(row_of(c * CH + k + 1), None, keep_h)
-        return carry
-
-    lax.fori_loop(0, NCH, grad_two, 0)
+
+    def after_g(i):
+        for c in range(PAIR * (i + 1) + 1, min(PAIR * (i + 2) + 1, NCH)):
+            grad_two(c)
+
+    for c in range(min(PAIR + 1, NCH)):
+        grad_two(c)
     for side in range(2):
         grad_rows(END[side] * R, keep_o[side], keep_ho[side])
 
@@ -835,13 +857,12 @@
             slopes.append(slope)
         return (plain, along), slopes
 
-    plain, along = paired(SLO1, back_step, (zero8, zero8))
+    plain, along = paired(SLO1, back_step, (zero8, zero8), after=after_g)
     stats_send(3, fold(one(plain)), fold(one(along)))
     send_late(SLO1)
     kernel_products(vt_a, vo_g, vh_g)
-    forward(SLO1, ODD[: NCH // 4])
+    forward(SLO1, HALF)
     kernel_terms(1)
-    forward(SLO1, ODD[NCH // 4 :])
     sums1 = stats_wait(3)
     arrive_all(SLO1)
     pieces_send(1, 0)

time: 60.9 us -> 59.6 us (0.979)
  Pallas kernels: 60.1 us -> 58.8 us
    pallas_call x1, Pallas kernels: 58.8 us -> 57.5 us  [local(): pl.pallas_call(functools.partial(kernel, nx, ny, total), name='blocks', o...]
where the time goes in v4:
time: 59.6 us; the launch traced here: 59.5 us
  Pallas kernels  58.8 us (99%)
  between operations  0.64 us (1%)
    pallas_call x1, Pallas kernels, local(): pl.pallas_call(functools.partial(kernel, nx, ny, total), name='blocks', o...  57.5 us
    pallas_call x1, Pallas kernels, local(): pl.pallas_call(finish, name='finish', out_shape=[volume, volume, terms, t...  1.3 us

profile of v4, /device:TPU:0, one launch (start us, length us, event | category | flops | bytes accessed | tf_op | source)
XLA Modules:
  0.0 59.5 jit_solution(16040186864727283963)
XLA Ops:
  0.6 57.5 %blocks.1 = (bf16[32,2,32,128]{3,2,1,0:T(8,128)(2,1)S(1)}, bf16[32,2,32,128]{3,2,1,0:T(8,128)(2,1)S(1)}, f32[27,32,32]{2,1,0:T(8,128)S(1)}, f32[27,32,32]{2,1,0:T(8,128)S(1)}, f32[4,32]{1,0:T(4,128)S(1)}) custom-call(bf16[32,2,32,128]{3,2,1,0:T(8,128)(2,1)} %f_hbm.1, bf16[32,2,32,128]{3,2,1,0:T(8,128)(2,1)} %c_hbm.1, bf16[27,32,32]{2,1,0:T(8,128)(2,1)} %bitcast.16, ...), custom_call_target="tpu_custom_call" | custom-call | tf_op jit(solution)/shard_map/blocks/pallas_call | solution.py:966
  58.2 1.3 %finish.1 = (bf16[32,2,32,128]{3,2,1,0:T(8,128)(2,1)}, bf16[32,2,32,128]{3,2,1,0:T(8,128)(2,1)}, f32[27,32,32]{2,1,0:T(8,128)}, f32[27,32,32]{2,1,0:T(8,128)}, f32[4,32]{1,0:T(4,128)}) custom-call(bf16[32,2,32,128]{3,2,1,0:T(8,128)(2,1)S(1)} %get-tuple-element.15.o_ref, bf16[32,2,32,128]{3,2,1,0:T(8,128)(2,1)S(1)} %get-tuple-element.16.fg_ref, ...), custom_call_target="tpu_custom_call" | custom-call | tf_op jit(solution)/shard_map/finish/pallas_call | solution.py:987

commit v5 on v4

--- a/solution.py
+++ b/solution.py
@@ -737,7 +737,6 @@
     forward(HID1, HALF)
     center, inv1 = moments(0)
     send_all(COT)
-    arrive_all(HID1)
 
     def put_a(n_dst, v_dst, inv, gain, bias, center):
         def use(row, value, mid, keep):
@@ -752,21 +751,27 @@
 
     halo_a = put_a(n1h, vh_a, inv1, gain1, bias1, center)
 
-    def active_chunk(c):
+    def active_own(c):
         mid = mcs1[c : c + 1, :]
         for k in range(CH):
             own_a(row_of(c * CH + k + 1), hc1[pl.ds(row_of(c * CH + k), R), :], mid, None)
+
+    def active_halo(c):
         found, mid = halo_rows(HID1, c)
         for k, value in enumerate(found):
             halo_a(row_of(c * CH + k + 1), value, mid, keep_h)
 
     def after_a(i):
         for c in range(PAIR * (i + 1) + 1, min(PAIR * (i + 2) + 1, NCH)):
-            active_chunk(c)
-
+            active_own(c)
+            active_halo(c)
+
+    for c in range(min(PAIR + 1, NCH)):
+        active_own(c)
+    arrive_all(HID1)
     each_end(HID1, halo_a, own_a)
     for c in range(min(PAIR + 1, NCH)):
-        active_chunk(c)
+        active_halo(c)
 
     mean, spread = forward_loop(vo_a, vh_a, wf2, HID2, after=after_a)
     stats_send(1, mean, spread)
@@ -797,7 +802,6 @@
     forward(HID2, HALF)
     leave(outb, o_ref)
     arrive_all(COT)
-    arrive_all(HID2)
 
     def put_c(dst):
         def use(row, value, mid, keep):
@@ -816,6 +820,7 @@
 
         return use
 
+    arrive_all(HID2)
     each_halo(HID2, put_s(n2h, s2h, vh_c), put_s(n2o, s2o, vo_c))
     sums2 = stats_wait(2)
 
@@ -864,8 +869,6 @@
     forward(SLO1, HALF)
     kernel_terms(1)
     sums1 = stats_wait(3)
-    arrive_all(SLO1)
-    pieces_send(1, 0)
     factor1 = gain1 * inv1
 
     def put_g(dst, normed_ref):
@@ -883,6 +886,8 @@
         return carry
 
     lax.fori_loop(0, NCH, grad_one, 0)
+    pieces_send(1, 0)
+    arrive_all(SLO1)
     each_halo(SLO1, put_g(vh_g, n1h), put_g(vo_g, n1o))
     kernel_products(vt_f, vo_g, vh_g)
     kernel_terms(0)

time: 59.6 us -> 59.1 us (level)
  no operation moved by 1% of the time
where the time goes in v5:
time: 59.1 us; the launch traced here: 59 us
  Pallas kernels  58.3 us (99%)
  between operations  0.64 us (1%)
    pallas_call x1, Pallas kernels, local(): pl.pallas_call(functools.partial(kernel, nx, ny, total), name='blocks', o...  57 us
    pallas_call x1, Pallas kernels, local(): pl.pallas_call(finish, name='finish', out_shape=[volume, volume, terms, t...  1.3 us

profile of v5, /device:TPU:0, one launch (start us, length us, event | category | flops | bytes accessed | tf_op | source)
XLA Modules:
  0.0 59.0 jit_solution(10992785226106348032)
XLA Ops:
  0.6 57.0 %blocks.1 = (bf16[32,2,32,128]{3,2,1,0:T(8,128)(2,1)S(1)}, bf16[32,2,32,128]{3,2,1,0:T(8,128)(2,1)S(1)}, f32[27,32,32]{2,1,0:T(8,128)S(1)}, f32[27,32,32]{2,1,0:T(8,128)S(1)}, f32[4,32]{1,0:T(4,128)S(1)}) custom-call(bf16[32,2,32,128]{3,2,1,0:T(8,128)(2,1)} %f_hbm.1, bf16[32,2,32,128]{3,2,1,0:T(8,128)(2,1)} %c_hbm.1, bf16[27,32,32]{2,1,0:T(8,128)(2,1)} %bitcast.16, ...), custom_call_target="tpu_custom_call" | custom-call | tf_op jit(solution)/shard_map/blocks/pallas_call | solution.py:971
  57.7 1.3 %finish.1 = (bf16[32,2,32,128]{3,2,1,0:T(8,128)(2,1)}, bf16[32,2,32,128]{3,2,1,0:T(8,128)(2,1)}, f32[27,32,32]{2,1,0:T(8,128)}, f32[27,32,32]{2,1,0:T(8,128)}, f32[4,32]{1,0:T(4,128)}) custom-call(bf16[32,2,32,128]{3,2,1,0:T(8,128)(2,1)S(1)} %get-tuple-element.15.o_ref, bf16[32,2,32,128]{3,2,1,0:T(8,128)(2,1)S(1)} %get-tuple-element.16.fg_ref, ...), custom_call_target="tpu_custom_call" | custom-call | tf_op jit(solution)/shard_map/finish/pallas_call | solution.py:992
